TPU v7x, 32 devices: a whole 2x2x4 slice. The times are simulated.
32 devices in a mesh: dp: 4 (over z), expert: 4 (over y, x), tensor: 2 (over core).
Axes of the slice: x: 2, y: 2, z: 4, core: 2. Of those that a mesh axis runs over, the one named last changes fastest.
Arguments:
- tokens: bfloat16 [192, 7168], P(('dp', 'expert')), may hold values from -6 to 6
- expert_ids: int32 [192, 8], P(('dp', 'expert')), may hold values from 0 to 15, all different within a row; in each aligned block of 12 rows (0 to 11, 12 to 23, ...) at most 8 rows name the same one
- route_weights: float32 [192, 8], P(('dp', 'expert')), may hold values from 0.1 to 1
- gate_weights: bfloat16 [16, 7168, 2048], P('expert', 'dp', 'tensor'), may hold values from -0.0625 to 0.0625
- up_weights: bfloat16 [16, 7168, 2048], P('expert', 'dp', 'tensor'), may hold values from -0.0625 to 0.0625
- down_weights: bfloat16 [16, 2048, 7168], P('expert', 'tensor', 'dp'), may hold values from -0.125 to 0.125
- shared_gate: bfloat16 [7168, 2048], P('dp', 'tensor'), may hold values from -0.0625 to 0.0625
- shared_up: bfloat16 [7168, 2048], P('dp', 'tensor'), may hold values from -0.0625 to 0.0625
- shared_down: bfloat16 [2048, 7168], P('tensor', 'dp'), may hold values from -0.125 to 0.125
Outputs:
- mixed: bfloat16 [192, 7168], P(('dp', 'expert'))
Inputs may be any that keep to these rules, and one draw needn't show every extreme that they name: `expert_ids`: each token names 8 different experts. In the rows of one device no expert is named by more than 8 tokens, and in some device's rows some expert is named by exactly 8.
All inputs are finite; a program needn't handle non-finite values.
Results may differ from a plain program's by a relative error of at most 0.005.
Values may be sent and summed in bfloat16 or wider, within the bound.
A program may use at most 128 MiB of HBM per device.

v0:
```python
import functools

import jax
import jax.numpy as jnp
from jax import lax
from jax.experimental import pallas as pl
from jax.experimental.pallas import tpu as pltpu
from jax.sharding import PartitionSpec as P

CAP = 8
STEPS = 8
MESH = pl.DeviceIdType.MESH
VMEM = pl.BlockSpec(memory_space=pltpu.VMEM)
DMA = pltpu.SemaphoreType.DMA


def greet(peers):
    barrier = pltpu.get_barrier_semaphore()
    for peer in peers:
        pl.semaphore_signal(barrier, inc=1, device_id=peer, device_id_type=MESH)
    pl.semaphore_wait(barrier, len(peers))


def remote(src, dst, send, recv, peer):
    return pltpu.make_async_remote_copy(
        src_ref=src, dst_ref=dst, send_sem=send, recv_sem=recv, device_id=peer, device_id_type=MESH
    )


def params(number):
    return pltpu.CompilerParams(
        collective_id=number, has_side_effects=True, vmem_limit_bytes=60 * 1024 * 1024
    )


def squared(v):
    return v * jnp.abs(v)


def rooted(v):
    v = v.astype(jnp.float32)
    root = jnp.sqrt(jnp.abs(v))
    return jnp.where(v < 0.0, -root, root)


def dispatch_kernel(n, g, tok, coef, x, w, own, s1, r1, s2, r2):
    d, e = lax.axis_index("dp"), lax.axis_index("expert")
    greet(
        [{"dp": lax.rem(d + k, n)} for k in range(1, n)]
        + [{"expert": lax.rem(e + j, g)} for j in range(1, g)]
    )
    mine = [
        pltpu.make_async_copy(tok.at[d], x.at[d, e], own.at[0]),
        pltpu.make_async_copy(coef, w.at[d, e], own.at[1]),
    ]
    for copy in mine:
        copy.start()
    sends = []
    for k in range(1, n):
        to = lax.rem(d + k, n)
        for src, dst, a in ((tok.at[to], x.at[d, e], 0), (coef, w.at[d, e], 1)):
            copy = remote(src, dst, s1.at[a, k], r1.at[a, k], {"dp": to})
            copy.start()
            sends.append(copy)
    for k in range(n):
        block = lax.rem(d - k + n, n)
        for a, ref in ((0, x), (1, w)):
            if k == 0:
                mine[a].wait()
            else:
                remote(ref.at[block, e], ref.at[block, e], s1.at[a, k], r1.at[a, k], {"dp": d}).wait_recv()
            for j in range(1, g):
                copy = remote(
                    ref.at[block, e], ref.at[block, e], s2.at[a, k, j], r2.at[a, k, j],
                    {"expert": lax.rem(e + j, g)},
                )
                copy.start()
                sends.append(copy)
    for k in range(n):
        block = lax.rem(d - k + n, n)
        for a, ref in ((0, x), (1, w)):
            for j in range(1, g):
                at = ref.at[block, lax.rem(e - j + g, g)]
                remote(at, at, s2.at[a, k, j], r2.at[a, k, j], {"expert": e}).wait_recv()
    for copy in sends:
        copy.wait_send()


def dispatch(blocks, coef, n, g):
    return pl.pallas_call(
        functools.partial(dispatch_kernel, n, g),
        out_shape=(
            jax.ShapeDtypeStruct((n, g) + blocks.shape[1:], blocks.dtype),
            jax.ShapeDtypeStruct((n, g) + coef.shape, coef.dtype),
        ),
        in_specs=[VMEM] * 2,
        out_specs=(VMEM, VMEM),
        scratch_shapes=[
            DMA((2,)), DMA((2, n)), DMA((2, n)), DMA((2, n, g)), DMA((2, n, g)),
        ],
        compiler_params=params(0),
    )(blocks, coef)


def chain_kernel(
    n, steps, gate, up, scale, sgate, sup, hid, shid,
    got, out, sgot, sout, s1, r1, s2, r2, t1, q1, t2, q2,
):
    d = lax.axis_index("dp")
    prev, after = lax.rem(d - 1 + n, n), lax.rem(d + 1, n)
    greet([{"dp": prev}, {"dp": after}])
    place = (d, n - 1 - d)
    ahead = (jnp.minimum(d + 1, n - 1), jnp.maximum(d - 1, 0))
    behind = (jnp.maximum(d - 1, 0), jnp.minimum(d + 1, n - 1))

    routed = ((gate, up), got, out, hid, s1, r1, s2, r2)
    shared = ((sgate, sup), sgot, sout, shid, t1, q1, t2, q2)

    def partial_send(group, i, src, way):
        parts, got_, out_, hid_, sa, ra, sb, rb = group
        return [remote(src[h], got_.at[h, i], sa.at[h, i], ra.at[h, i], {"dp": ahead[way]}) for h in (0, 1)]

    def hidden_send(group, i, way):
        hid_, sb, rb = group[3], group[6], group[7]
        return remote(hid_.at[i], hid_.at[i], sb.at[i], rb.at[i], {"dp": behind[way]})

    def first(group, i, way):
        @pl.when(place[way] == 0)
        def _():
            for copy in partial_send(group, i, [part.at[i] for part in group[0]], way):
                copy.start()

    def forward(group, i, way, factor):
        parts, got_, out_, hid_ = group[:4]

        @pl.when(place[way] > 0)
        def _():
            for copy in partial_send(group, i, [got_.at[h, i] for h in (0, 1)], way):
                copy.wait_recv()
            sums = [rooted(parts[h][i]) + rooted(got_[h, i]) for h in (0, 1)]

            @pl.when(place[way] < n - 1)
            def _():
                for h in (0, 1):
                    out_[h, i] = squared(sums[h]).astype(out_.dtype)
                for copy in partial_send(group, i, [out_.at[h, i] for h in (0, 1)], way):
                    copy.start()

            @pl.when(place[way] == n - 1)
            def _():
                value = sums[0] / (1.0 + jnp.exp(-sums[0])) * sums[1]
                if factor is not None:
                    value = value * factor[i]
                hid_[i] = value.astype(hid_.dtype)
                hidden_send(group, i, way).start()

    def spread(group, i, way):
        hidden_send(group, i, way).wait_recv()

        @pl.when(place[way] > 0)
        def _():
            hidden_send(group, i, way).start()

    for s in range(steps):
        for way in (0, 1):
            first(routed, 2 * s + way, way)
    for way in (0, 1):
        first(shared, way, way)

    total = steps + 1
    for s in range(total + 2 * (n - 1)):
        for way in (0, 1):
            if s < steps:
                forward(routed, 2 * s + way, way, scale)
            elif s == steps:
                forward(shared, way, way, None)
            late = s - 2 * (n - 1 - place[way])

            @pl.when((place[way] < n - 1) & (late >= 0) & (late < steps))
            def _():
                spread(routed, 2 * late + way, way)

            @pl.when((place[way] < n - 1) & (late == steps))
            def _():
                spread(shared, way, way)

    def finish(group, i, way):
        parts, got_, out_ = group[:3]

        @pl.when(place[way] < n - 1)
        def _():
            for copy in partial_send(group, i, [out_.at[h, i] for h in (0, 1)], way):
                copy.wait_send()

        @pl.when(place[way] > 0)
        def _():
            hidden_send(group, i, way).wait_send()

    for s in range(steps):
        for way in (0, 1):
            finish(routed, 2 * s + way, way)
    for way in (0, 1):
        finish(shared, way, way)


def chain(gate, up, scale, sgate, sup, n):
    pieces, rows, width = gate.shape
    half, thin = sgate.shape[1:]
    wire = gate.dtype
    return pl.pallas_call(
        functools.partial(chain_kernel, n, pieces // 2),
        out_shape=(
            jax.ShapeDtypeStruct((pieces, rows, width), jnp.bfloat16),
            jax.ShapeDtypeStruct((2, half, thin), jnp.bfloat16),
        ),
        in_specs=[VMEM] * 5,
        out_specs=(VMEM, VMEM),
        scratch_shapes=[
            pltpu.VMEM((2, pieces, rows, width), wire),
            pltpu.VMEM((2, pieces, rows, width), wire),
            pltpu.VMEM((2, 2, half, thin), wire),
            pltpu.VMEM((2, 2, half, thin), wire),
            DMA((2, pieces)), DMA((2, pieces)), DMA((pieces,)), DMA((pieces,)),
            DMA((2, 2)), DMA((2, 2)), DMA((2,)), DMA((2,)),
        ],
        compiler_params=params(1),
    )(gate, up, scale, sgate, sup)


def collect_kernel(n, g, y, o, peer_in, z, plane, done, sa, ra, sb, rb, sc, rc, own):
    d, e, t = lax.axis_index("dp"), lax.axis_index("expert"), lax.axis_index("tensor")
    other = 1 - t
    half = n // 2
    greet(
        [{"tensor": other}]
        + [{"expert": lax.rem(e + j, g)} for j in range(1, g)]
        + [{"dp": lax.rem(d + k, n), "tensor": c} for k in range(1, n) for c in (0, 1)]
    )
    swap = []
    for j in range(g):
        to = lax.rem(e + j, g)
        copy = remote(
            y.at[pl.ds(other * half, half), to], peer_in.at[to], sa.at[j], ra.at[j], {"tensor": other}
        )
        copy.start()
        swap.append(copy)
    sends = []
    for j in list(range(1, g)) + [0]:
        to = lax.rem(e + j, g)
        swap[j].wait_recv()
        z[to] = y[pl.ds(t * half, half), to] + peer_in[to]
        if j:
            copy = remote(z.at[to], plane.at[j], sb.at[j], rb.at[j], {"expert": to})
            copy.start()
            sends.append(copy)
    total = z[e]
    for j in range(1, g):
        sends[j - 1].wait_recv()
        total = total + plane[j]
    done[...] = total.astype(done.dtype)
    last = []
    for i in range(half):
        home = t * half + i
        for c in (0, 1):
            here = (home == d) & (t == c)
            away = remote(
                done.at[i], o.at[d], sc.at[i, c], rc.at[d], {"dp": home, "tensor": c}
            )
            pl.when(jnp.logical_not(here))(away.start)
            local = pltpu.make_async_copy(done.at[i], o.at[d], own)
            pl.when(here)(local.start)
            last.append((here, away, local))
    for k in range(n):
        local_arrives = (d // half == t) & (d == k)

        @pl.when(jnp.logical_not(local_arrives))
        def _():
            remote(done.at[0], o.at[k], sc.at[0, 0], rc.at[k], {"dp": d}).wait_recv()

    for here, away, local in last:
        pl.when(jnp.logical_not(here))(away.wait_send)
        pl.when(here)(local.wait)
    for copy in swap + sends:
        copy.wait_send()


def collect(y, n, g):
    rows, width = y.shape[2:]
    half = n // 2
    return pl.pallas_call(
        functools.partial(collect_kernel, n, g),
        out_shape=jax.ShapeDtypeStruct((n, rows, width), jnp.bfloat16),
        in_specs=[VMEM],
        out_specs=VMEM,
        scratch_shapes=[
            pltpu.VMEM((g, half, rows, width), jnp.float32),
            pltpu.VMEM((g, half, rows, width), jnp.float32),
            pltpu.VMEM((g, half, rows, width), jnp.float32),
            pltpu.VMEM((half, rows, width), jnp.bfloat16),
            DMA((g,)), DMA((g,)), DMA((g,)), DMA((g,)), DMA((half, 2)), DMA((n,)), DMA,
        ],
        compiler_params=params(2),
    )(y)


def per_device(
    tokens, expert_ids, route_weights, gate_weights, up_weights, down_weights,
    shared_gate, shared_up, shared_down,
):
    g, n = lax.axis_size("expert"), lax.axis_size("dp")
    e = lax.axis_index("expert")
    rows, model = tokens.shape
    local, width, hidden = gate_weights.shape
    experts = local * g
    blocks = n * g
    count = blocks * rows
    wire = jnp.bfloat16 if n <= 4 else jnp.float32

    names = jnp.arange(experts, dtype=jnp.int32)
    coef = jnp.sum(
        jnp.where(expert_ids[:, :, None] == names, route_weights[:, :, None], 0.0), axis=1
    )
    x, w = dispatch(tokens.reshape(rows, n, width).transpose(1, 0, 2), coef, n, g)
    x = x.reshape(count, width)
    own = lax.dynamic_slice_in_dim(w.reshape(blocks, rows, experts), e * local, local, 2)
    chosen = own > 0.0
    order = jnp.tril(jnp.ones((rows, rows), jnp.float32), -1)
    place = jnp.einsum("ij,bjl->bil", order, chosen.astype(jnp.float32)).astype(jnp.int32)
    place = jnp.where(chosen, place, CAP).reshape(count, local)
    slot = jnp.arange(blocks * CAP, dtype=jnp.int32)
    block_of = jnp.arange(count, dtype=jnp.int32) // rows
    target = block_of[:, None] * CAP + place
    hit = (place < CAP).T[:, None, :] & (target.T[:, None, :] == slot[None, :, None])
    pick = hit.astype(jnp.bfloat16)
    scale = jnp.sum(jnp.where(hit, own.reshape(count, local).T[:, None, :], 0.0), axis=2)

    picked = jnp.einsum("lrt,td->lrd", pick, x, preferred_element_type=jnp.float32).astype(jnp.bfloat16)
    gate = squared(jnp.einsum("lrd,ldf->lrf", picked, gate_weights, preferred_element_type=jnp.float32)).astype(wire)
    up = squared(jnp.einsum("lrd,ldf->lrf", picked, up_weights, preferred_element_type=jnp.float32)).astype(wire)
    thin = hidden // g
    my_gate = lax.dynamic_slice_in_dim(shared_gate, e * thin, thin, 1)
    my_up = lax.dynamic_slice_in_dim(shared_up, e * thin, thin, 1)
    sgate = squared(jnp.dot(x, my_gate, preferred_element_type=jnp.float32)).astype(wire)
    sup = squared(jnp.dot(x, my_up, preferred_element_type=jnp.float32)).astype(wire)

    pieces = 2 * STEPS
    tall = local * blocks * CAP // pieces
    hid, shid = chain(
        gate.reshape(pieces, tall, hidden), up.reshape(pieces, tall, hidden),
        scale.reshape(pieces, tall, 1),
        sgate.reshape(2, count // 2, thin), sup.reshape(2, count // 2, thin), n,
    )
    hid = hid.reshape(local, blocks * CAP, hidden)
    shid = shid.reshape(count, thin)
    spread = jnp.einsum("lrt,lrf->tlf", pick, hid, preferred_element_type=jnp.float32).astype(jnp.bfloat16)
    my_down = lax.dynamic_slice_in_dim(shared_down, e * thin, thin, 0)
    y = jnp.dot(
        spread.reshape(count, local * hidden), down_weights.reshape(local * hidden, width),
        preferred_element_type=jnp.float32,
    ) + jnp.dot(shid, my_down, preferred_element_type=jnp.float32)
    o = collect(y.reshape(n, g, rows, width), n, g)
    return o.transpose(1, 0, 2).reshape(rows, model)


def solution(mesh):
    placed = (
        P(("dp", "expert"), None),
        P(("dp", "expert"), None),
        P(("dp", "expert"), None),
        P("expert", "dp", "tensor"),
        P("expert", "dp", "tensor"),
        P("expert", "tensor", "dp"),
        P("dp", "tensor"),
        P("dp", "tensor"),
        P("tensor", "dp"),
    )
    return jax.shard_map(
        per_device, mesh=mesh, in_specs=placed, out_specs=P(("dp", "expert"), None), check_vma=False
    )
```

profile of v0, /device:TPU:0, one launch (start us, length us, event | category | flops | bytes accessed | tf_op | source)
XLA Modules:
  0.0 202.8 jit_solution(7880081497566514449)
XLA Ops:
  0.0 0.8 copy.20
  0.8 0.8 copy.21
  1.6 0.7 select_reduce_fusion.1.coef
  2.2 1.0 reshape.64
  3.3 0.7 copy.28
  4.0 21.9 %shard_map.91 = (bf16[4,4,12,1792]{3,2,1,0:T(8,128)(2,1)}, f32[4,4,12,16]{3,2,1,0:T(8,128)}) custom-call(bf16[4,12,1792]{2,1,0:T(8,128)(2,1)} %bitcast.48, f32[12,16]{1,0:T(8,128)} %select_reduce_fusion.1.coef), custom_call_target="tpu_custom_call" | custom-call | tf_op jit(solution)/shard_map/pallas_call | solution.py:90
  25.9 1.0 constant_dynamic-slice_fusion
  26.9 0.2 copy.25
  27.1 0.1 reshape.70
  27.2 0.2 fusion.4
  27.4 0.1 reshape.66
  27.5 0.4 select_reduce_fusion
  27.9 0.9 reshape.82.scale
  28.8 1.3 reshape.67
  30.1 1.3 reshape.79
  31.4 2.2 %fusion.21 = bf16[192,256]{1,0:T(8,128)(2,1)} fusion(bf16[192,1792]{1,0:T(8,128)(2,1)S(1)} %reshape.67, bf16[1792,1024]{1,0:T(8,128)(2,1)} %param.15, s32[]{:T(128)S(6)} %select_n.39), kind=kOutput, calls=%fused_computation.23 | convolution fusion | flops 176308224 | bytes 1703940 | tf_op jit(solution)/shard_map/dot_general | solution.py:343
  33.6 2.2 %fusion.16 = bf16[192,256]{1,0:T(8,128)(2,1)} fusion(bf16[192,1792]{1,0:T(8,128)(2,1)S(1)} %reshape.67, bf16[1792,1024]{1,0:T(8,128)(2,1)} %param.16, s32[]{:T(128)S(6)} %select_n.39), kind=kOutput, calls=%fused_computation.21 | convolution fusion | flops 176308224 | bytes 1703940 | tf_op jit(solution)/shard_map/dot_general | solution.py:344
  35.8 1.0 convolution_convert_fusion
  36.8 0.0 copy-start
  36.8 8.5 %fusion.1 = bf16[4,128,1024]{2,1,0:T(8,128)(2,1)} fusion(bf16[4,128,1792]{2,1,0:T(8,128)(2,1)S(1)} %convolution_convert_fusion, bf16[4,1792,1024]{2,1,0:T(8,128)(2,1)} %param.13), kind=kOutput, calls=%fused_computation.6 | convolution fusion | flops 1880621056 | bytes 17563648 | tf_op jit(solution)/shard_map/lrd,ldf->lrf/dot_general | solution.py:339
  45.3 1.2 copy-done
  46.5 3.1 %fusion = bf16[4,128,1024]{2,1,0:T(8,128)(2,1)} fusion(bf16[4,128,1792]{2,1,0:T(8,128)(2,1)S(1)} %convolution_convert_fusion, bf16[4,1792,1024]{2,1,0:T(8,128)(2,1)S(1)} %copy-done), kind=kOutput, calls=%fused_computation.5 | convolution fusion | flops 1880621056 | bytes 17563648 | tf_op jit(solution)/shard_map/lrd,ldf->lrf/dot_general | solution.py:338
  49.6 114.7 %shard_map.92 = (bf16[16,32,1024]{2,1,0:T(8,128)(2,1)}, bf16[2,96,256]{2,1,0:T(8,128)(2,1)}) custom-call(bf16[16,32,1024]{2,1,0:T(8,128)(2,1)} %bitcast.46, bf16[16,32,1024]{2,1,0:T(8,128)(2,1)} %bitcast.45, f32[16,32,1]{2,1,0:T(8,128)} %reshape.82.scale, bf16[2,96,256]{2,1,0:T(8,128)(2,1)} %bitcast.50, bf16[2,96,256]{2,1,0:T(8,128)(2,1)} %bitcast.51), custom_call_target="tpu_custom_call" | custom-call | tf_op jit(solution)/shard_map/pallas_call | solution.py:210
  164.3 0.0 copy-start.1
  164.3 9.1 %convolution_bitcast_fusion = f32[192,1792]{1,0:T(8,128)S(1)} fusion(bf16[4,1024,1792]{2,1,0:T(8,128)(2,1)} %param.14, bf16[4,128,1024]{2,1,0:T(8,128)(2,1)} %bitcast.55, s32[4,192]{1,0:T(4,128)S(1)} %add_bitcast_fusion, pred[4,192]{1,0:T(4,128)(4,1)S(1)} %compare_bitcast_fusion), kind=kOutput, calls=%fused_computation.4 | convolution fusion | flops 3020881920 | bytes 17108736 | tf_op jit(solution)/shard_map/dot_general | solution.py:357
  173.4 0.0 copy-done.1
  173.4 1.5 convolution_add_fusion
  175.0 1.4 reshape.76.y
  176.4 24.6 %shard_map.93 = bf16[4,12,1792]{2,1,0:T(8,128)(2,1)} custom-call(f32[4,4,12,1792]{3,2,1,0:T(8,128)} %reshape.76.y), custom_call_target="tpu_custom_call" | custom-call | tf_op jit(solution)/shard_map/pallas_call | solution.py:290
  201.0 1.0 copy.24
  202.0 0.1 pad
  202.1 0.7 copy.26
  (4 shorter events, 0.0 us)
Async XLA Ops:
  36.8 9.7 %copy-start = (bf16[4,1792,1024]{2,1,0:T(8,128)(2,1)S(1)}, bf16[4,1792,1024]{2,1,0:T(8,128)(2,1)}, u32[]{:S(2)}) copy-start(bf16[4,1792,1024]{2,1,0:T(8,128)(2,1)} %param.12) | copy-start | bytes 44040196
  164.3 9.1 %copy-start.1 = (bf16[2,96,256]{2,1,0:T(8,128)(2,1)S(1)}, bf16[2,96,256]{2,1,0:T(8,128)(2,1)}, u32[]{:S(2)}) copy-start(bf16[2,96,256]{2,1,0:T(8,128)(2,1)} %get-tuple-element.12) | copy-start | bytes 294916
where the time goes:
time: 204 us; the launch traced here: 203 us
  Pallas kernels  161 us (79%)
  matrix products  27.8 us (14%)
  local copies, waits for them, and re-layouts  12.6 us (6%)
    pallas_call x1, Pallas kernels, chain(): pl.pallas_call(functools.partial(chain_kernel, n, pieces // 2), out_shape...  115 us
    pallas_call x1, Pallas kernels, collect(): pl.pallas_call(functools.partial(collect_kernel, n, g), out_shape=jax.Sha...  24.6 us
    pallas_call x1, Pallas kernels, dispatch(): pl.pallas_call(functools.partial(dispatch_kernel, n, g), out_shape=(jax.S...  21.9 us
    dot_general x1, matrix products, per_device(): jnp.dot(spread.reshape(count, local * hidden), down_weights.reshape(local...  9.08 us
    dot_general x1, matrix products, per_device(): jnp.einsum('lrd,ldf->lrf', picked, up_weights, preferred_element_type=jnp...  8.55 us

commit v1 on v0

v1 whole, which is shorter than its diff:
```python
import functools

import jax
import jax.numpy as jnp
from jax import lax
from jax.experimental import pallas as pl
from jax.experimental.pallas import tpu as pltpu
from jax.sharding import PartitionSpec as P

CAP = 8
PITCH = 16
TILE = 256
COLS = 256
ROWS = 64
AHEAD = 3
SKEW = 2
SPREAD_SKEW = 2
MESH = pl.DeviceIdType.MESH
VMEM = pl.BlockSpec(memory_space=pltpu.VMEM)
HBM = pl.BlockSpec(memory_space=pl.ANY)
DMA = pltpu.SemaphoreType.DMA
F32 = jnp.float32
BF16 = jnp.bfloat16


def greet(peers):
    barrier = pltpu.get_barrier_semaphore()
    for peer in peers:
        pl.semaphore_signal(barrier, inc=1, device_id=peer, device_id_type=MESH)
    pl.semaphore_wait(barrier, len(peers))


def remote(src, dst, send, recv, peer):
    return pltpu.make_async_remote_copy(
        src_ref=src, dst_ref=dst, send_sem=send, recv_sem=recv, device_id=peer, device_id_type=MESH
    )


def params(number, limit=60 * 1024 * 1024):
    return pltpu.CompilerParams(
        collective_id=number, has_side_effects=True, vmem_limit_bytes=limit
    )


def packed(v, wire):
    return v if wire == F32 else (v * jnp.abs(v)).astype(wire)


def unpacked(v):
    if v.dtype == F32:
        return v
    v = v.astype(F32)
    size = jnp.abs(v)
    root = size * lax.rsqrt(jnp.maximum(size, 1e-30))
    return jnp.where(v < 0.0, -root, root)


def dot(a, b):
    return jnp.dot(a, b, preferred_element_type=F32)


def dispatch_kernel(n, g, tok, ids, weights, x, w, coef, own, s1, r1, s2, r2, s3, r3):
    d, e, t = lax.axis_index("dp"), lax.axis_index("expert"), lax.axis_index("tensor")
    width, experts = x.shape[3], w.shape[3]
    split = (width // 2) % 128 == 0
    half = width // 2 if split else width
    lanes = pl.ds(pl.multiple_of(t * half, 128), half) if split else pl.ds(0, width)

    def columns(block, part):
        start = block * width + (t * half if part and split else 0)
        return tok.at[:, pl.ds(pl.multiple_of(start, 128), half if part else width)]

    mine = pltpu.make_async_copy(columns(d, False), x.at[d, e], own.at[0])
    mine.start()
    name = lax.broadcasted_iota(jnp.int32, coef.shape, 1)
    total = jnp.zeros(coef.shape, F32)
    for k in range(ids.shape[1]):
        total = total + jnp.where(ids[:, k:k + 1] == name, weights[:, k:k + 1], 0.0)
    coef[...] = total
    greet(
        [{"dp": lax.rem(d + k, n)} for k in range(1, n)]
        + [{"expert": lax.rem(e + j, g)} for j in range(1, g)]
        + [{"tensor": 1 - t}]
    )
    put = pltpu.make_async_copy(coef, w.at[d, e], own.at[1])
    put.start()
    sends = []
    for k in range(1, n):
        to = lax.rem(d + k, n)
        for src, dst, a in ((columns(to, True), x.at[d, e, :, lanes], 0), (coef, w.at[d, e], 1)):
            copy = remote(src, dst, s1.at[a, k], r1.at[a, k], {"dp": to})
            copy.start()
            sends.append(copy)

    def view(a, block, peer):
        return x.at[block, peer, :, lanes] if a == 0 else w.at[block, peer]

    def cross(k, j, block, peer):
        at = x.at[block, peer, :, lanes]
        return remote(at, at, s3.at[k, j], r3.at[k, j], {"tensor": 1 - t})

    for k in range(n):
        block = lax.rem(d - k + n, n)
        for a in (0, 1):
            if k == 0:
                (mine, put)[a].wait()
            else:
                at = view(a, block, e)
                remote(at, at, s1.at[a, k], r1.at[a, k], {"dp": d}).wait_recv()
            for j in range(1, g):
                at = view(a, block, e)
                copy = remote(at, at, s2.at[a, k, j], r2.at[a, k, j], {"expert": lax.rem(e + j, g)})
                copy.start()
                sends.append(copy)
        if split and k:
            copy = cross(k, 0, block, e)
            copy.start()
            sends.append(copy)
    for k in range(n):
        block = lax.rem(d - k + n, n)
        for a in (0, 1):
            for j in range(1, g):
                peer = lax.rem(e - j + g, g)
                at = view(a, block, peer)
                remote(at, at, s2.at[a, k, j], r2.at[a, k, j], {"expert": e}).wait_recv()
                if a == 0 and split:
                    copy = cross(k, j, block, peer)
                    copy.start()
                    sends.append(copy)
    if split:
        other = pl.ds(pl.multiple_of((1 - t) * half, 128), half)
        for k in range(n):
            block = lax.rem(d - k + n, n)
            for j in range(g):
                if k or j:
                    at = x.at[block, lax.rem(e - j + g, g), :, other]
                    remote(at, at, s3.at[k, j], r3.at[k, j], {"tensor": t}).wait_recv()
    for copy in sends:
        copy.wait_send()


def dispatch(tokens, ids, weights, experts, n, g):
    rows, model = tokens.shape
    return pl.pallas_call(
        functools.partial(dispatch_kernel, n, g),
        out_shape=(
            jax.ShapeDtypeStruct((n, g, rows, model // n), tokens.dtype),
            jax.ShapeDtypeStruct((n, g, rows, experts), F32),
        ),
        in_specs=[VMEM] * 3,
        out_specs=(VMEM, VMEM),
        scratch_shapes=[
            pltpu.VMEM((rows, experts), F32),
            DMA((2,)), DMA((2, n)), DMA((2, n)), DMA((2, n, g)), DMA((2, n, g)),
            DMA((n, g)), DMA((n, g)),
        ],
        compiler_params=params(0),
    )(tokens, ids, weights)


def layer_kernel(
    n, g, sliced, x, w, gate, up, down, sgate, sup, sdown, y,
    xs, ws, gbuf, ubuf, dbuf, sgbuf, subuf, sdbuf, picked, compact, spread, sspread, acc, factor,
    own, got, out, hid, sown, sgot, sout, shid, here, there,
    wsem, dsem, ssem, s1, r1, s2, r2, t1, q1, t2, q2,
):
    d, e = lax.axis_index("dp"), lax.axis_index("expert")
    rows, width = x.shape[2:]
    experts = w.shape[3]
    local, hidden = gate.shape[0], gate.shape[2]
    thin = sgbuf.shape[1]
    wire = out.dtype
    tiles = xs.shape[0] // TILE
    slots = TILE // PITCH * CAP
    solid = TILE // PITCH * rows
    pairs = hidden // COLS // 2
    pieces = own.shape[1]
    blocks = local * pairs
    per = pieces // blocks
    prev, after = lax.rem(d - 1 + n, n), lax.rem(d + 1, n)
    place = (d, n - 1 - d)
    ahead = (jnp.minimum(d + 1, n - 1), jnp.maximum(d - 1, 0))
    behind = (jnp.maximum(d - 1, 0), jnp.minimum(d + 1, n - 1))

    def cut(c):
        return pl.ds(pl.multiple_of(c * COLS, COLS), COLS)

    def load(b):
        at = b // pairs
        wide = pl.ds(pl.multiple_of(lax.rem(b, pairs) * 2 * COLS, 2 * COLS), 2 * COLS)
        return [
            pltpu.make_async_copy(src.at[at, :, wide], dst.at[at, :, wide], wsem.at[h, b])
            for h, (src, dst) in enumerate(((gate, gbuf), (up, ubuf)))
        ]

    start = 0 if sliced else e * thin
    across = pl.ds(0, thin) if sliced else pl.ds(pl.multiple_of(start, thin), thin)
    extra = [
        pltpu.make_async_copy(sgate.at[:, across], sgbuf, ssem.at[0]),
        pltpu.make_async_copy(sup.at[:, across], subuf, ssem.at[1]),
        pltpu.make_async_copy(sdown.at[across, :], sdbuf, ssem.at[2]),
    ]
    lowers = [pltpu.make_async_copy(down.at[l], dbuf.at[l], dsem.at[l]) for l in range(local)]

    for copy in extra[:2]:
        copy.start()
    for b in range(min(AHEAD, blocks)):
        for copy in load(b):
            copy.start()

    greeted = pltpu.get_barrier_semaphore()
    for peer in (prev, after):
        pl.semaphore_signal(greeted, inc=1, device_id={"dp": peer}, device_id_type=MESH)

    xs[...] = jnp.zeros_like(xs)
    ws[...] = jnp.zeros_like(ws)
    for i in range(n):
        for j in range(g):
            at = (i * g + j) * PITCH
            xs[at:at + rows, :] = x[i, j]
            ws[at:at + rows, :] = w[i, j]

    def iota(shape, axis):
        return lax.broadcasted_iota(jnp.int32, shape, axis)

    token_row, token_col = iota((TILE, TILE), 0), iota((TILE, TILE), 1)
    same = token_row // PITCH == token_col // PITCH
    before = jnp.where(same & (token_row < token_col), 1.0, 0.0).astype(BF16)
    behind_in = jnp.where(same & (token_col < token_row), 1.0, 0.0).astype(BF16)
    spots = 16
    pick_rows = jnp.where(
        iota((spots, experts), 1) == e * local + iota((spots, experts), 0), 1.0, 0.0
    ).astype(BF16)
    base_row = iota((spots, TILE), 1) // PITCH * CAP
    base_col = iota((TILE, experts), 0) // PITCH * CAP
    for a in range(tiles):
        part = ws[a * TILE:(a + 1) * TILE, :]
        chosen = jnp.where(part > 0.0, 1.0, 0.0).astype(BF16)
        row = lax.dot_general(
            pick_rows, chosen, (((1,), (1,)), ((), ())), preferred_element_type=F32
        )
        rank_row = dot(row.astype(BF16), before).astype(jnp.int32)
        goal_row = jnp.where(row > 0.5, base_row + rank_row, -1)
        rank_col = dot(behind_in, chosen).astype(jnp.int32)
        goal_col = jnp.where(part > 0.0, base_col + rank_col, -1).astype(F32)
        for l in range(local):
            mark = iota((TILE, experts), 1) == e * local + l
            column = jnp.sum(jnp.where(mark, goal_col, 0.0), axis=1, keepdims=True)
            here[a, l] = jnp.where(
                goal_row[l:l + 1, :] == iota((slots, TILE), 0), 1.0, 0.0
            ).astype(BF16)
            there[a, l] = jnp.where(
                column.astype(jnp.int32) == iota((TILE, slots), 1), 1.0, 0.0
            ).astype(BF16)
            factor[l, a * TILE:(a + 1) * TILE, :] = jnp.sum(
                jnp.where(mark, part, 0.0), axis=1, keepdims=True
            )

    def solid_map(shape, slot_axis, token_axis):
        token, slot = iota(shape, token_axis), iota(shape, slot_axis)
        inside = token % PITCH
        return jnp.where(
            (inside < rows) & (token // PITCH * rows + inside == slot), 1.0, 0.0
        ).astype(BF16)

    rest = solid // 2
    pack_map = solid_map((solid, TILE), 0, 1)
    for a in range(tiles):
        compact[...] = dot(pack_map, xs[a * TILE:(a + 1) * TILE, :]).astype(BF16)
        if a == 0:
            for copy in extra[:2]:
                copy.wait()
        for h, buf in ((0, sgbuf), (1, subuf)):
            value = dot(compact[...], buf[...])
            for way in (0, 1):
                sown[way, 0, h, a * rest:(a + 1) * rest, :] = value[way * rest:(way + 1) * rest]

    pl.semaphore_wait(greeted, 2)

    routed = (own, got, out if wire == BF16 else own, hid, s1, r1, s2, r2)
    shared = (sown, sgot, sout if wire == BF16 else sown, shid, t1, q1, t2, q2)

    def partial_send(group, way, i):
        return remote(
            group[2].at[way, i], group[1].at[way, i], group[4].at[way, i], group[5].at[way, i],
            {"dp": ahead[way]},
        )

    def hidden_send(group, way, i):
        at = group[3].at[way, i]
        return remote(at, at, group[6].at[way, i], group[7].at[way, i], {"dp": behind[way]})

    def forward(group, way, i):
        mine, come, leave, final = group[:4]

        @pl.when(place[way] == 0)
        def _():
            if leave is not mine:
                for h in (0, 1):
                    leave[way, i, h] = packed(mine[way, i, h], wire)
            partial_send(group, way, i).start()

        @pl.when(place[way] > 0)
        def _():
            partial_send(group, way, i).wait_recv()

            @pl.when(place[way] < n - 1)
            def _():
                for h in (0, 1):
                    leave[way, i, h] = packed(mine[way, i, h] + unpacked(come[way, i, h]), wire)
                partial_send(group, way, i).start()

            @pl.when(place[way] == n - 1)
            def _():
                a, b = (mine[way, i, h] + unpacked(come[way, i, h]) for h in (0, 1))
                final[way, i] = (a / (1.0 + jnp.exp(-a)) * b).astype(final.dtype)
                hidden_send(group, way, i).start()

    def pass_on(group, way, i):
        hidden_send(group, way, i).wait_recv()

        @pl.when(place[way] > 0)
        def _():
            hidden_send(group, way, i).start()

    def project(b):
        at, c = b // pairs, lax.rem(b, pairs) * 2

        @pl.when(c == 0)
        def _():
            for a in range(tiles):
                picked[a] = dot(here[a, at], xs[a * TILE:(a + 1) * TILE, :]).astype(BF16)

        for copy in load(b):
            copy.wait()

        @pl.when(b + AHEAD < blocks)
        def _():
            for copy in load(b + AHEAD):
                copy.start()

        @pl.when(b + AHEAD == blocks)
        def _():
            for copy in extra[2:] + lowers:
                copy.start()

        fine = slots // ROWS
        for way in (0, 1):
            for h, buf in ((0, gbuf), (1, ubuf)):
                for a in range(tiles):
                    value = dot(picked[a], buf[at, :, cut(c + way)])
                    for r in range(fine):
                        own[way, b * per + a * fine + r, h] = value[r * ROWS:(r + 1) * ROWS]

    def stage(b, carry):
        @pl.when(b < blocks)
        def _():
            project(b)

        for r in range(per):
            s = b * per + r
            for way in (0, 1):
                @pl.when(s == SKEW * place[way])
                def _():
                    forward(shared, way, 0)

                i = s - SKEW * place[way]

                @pl.when((i >= 0) & (i < pieces))
                def _():
                    forward(routed, way, i)
        return carry

    lax.fori_loop(0, blocks + -(-SKEW * (n - 1) // per), stage, 0)

    part_of = TILE if width % TILE == 0 else 128
    chunks = width // part_of
    ready = []

    def gather(l):
        for way in (0, 1):
            for c in range(pairs):
                b = l * pairs + c
                fine = slots // ROWS
                for a in range(tiles):
                    value = hid[way, b * per + a * fine:b * per + (a + 1) * fine]
                    spread[a * TILE:(a + 1) * TILE, (2 * c + way) * COLS:(2 * c + way + 1) * COLS] = dot(
                        there[a, l], value.reshape(slots, COLS)
                    ).astype(BF16)

    def shared_gather():
        unpack_map = solid_map((TILE, solid), 1, 0)
        for a in range(tiles):
            value = jnp.concatenate([shid[way, 0, a * rest:(a + 1) * rest] for way in (0, 1)], axis=0)
            sspread[a * TILE:(a + 1) * TILE, :] = dot(unpack_map, value).astype(BF16)

    def shared_down(c):
        at = slice(c * part_of, (c + 1) * part_of)
        for a in range(tiles):
            span = slice(a * TILE, (a + 1) * TILE)
            acc[span, at] = dot(sspread[span, :], sdbuf[:, at])

    def routed_down(l, c):
        at = slice(c * part_of, (c + 1) * part_of)
        for a in range(tiles):
            span = slice(a * TILE, (a + 1) * TILE)
            acc[span, at] += factor[l, span, :] * dot(spread[span, :], dbuf[l, :, at])

    def flush(c):
        at = slice(c * part_of, (c + 1) * part_of)
        for i in range(n):
            for j in range(g):
                top = (i * g + j) * PITCH
                y[i, j, :, at] = acc[top:top + rows, at]

    lag = SPREAD_SKEW * (n - 2)
    each = pieces // local
    for s in range(pieces + lag):
        for way in (0, 1):
            late = n - 2 - place[way]

            @pl.when((late >= 0) & (s == SPREAD_SKEW * late))
            def _():
                pass_on(shared, way, 0)

            i = s - SPREAD_SKEW * late

            @pl.when((late >= 0) & (i >= 0) & (i < pieces))
            def _():
                pass_on(routed, way, i)
        if s == lag:
            def _start():
                extra[2].wait()
                shared_gather()
            ready.append(_start)
            ready += [functools.partial(shared_down, c) for c in range(chunks)]
        if s >= lag and (s - lag + 1) % each == 0:
            l = (s - lag + 1) // each - 1

            def _begin(l=l):
                lowers[l].wait()
                gather(l)
            ready.append(_begin)
            for c in range(chunks):
                ready.append(functools.partial(routed_down, l, c))
                if l == local - 1:
                    ready.append(functools.partial(flush, c))
        quota = 3 if s < pieces + lag - 1 else len(ready)
        for task in ready[:quota]:
            task()
        ready = ready[quota:]

    def finish(group, way, i):
        @pl.when(place[way] < n - 1)
        def _():
            partial_send(group, way, i).wait_send()

        @pl.when(place[way] > 0)
        def _():
            hidden_send(group, way, i).wait_send()

    def drain(i, carry):
        for way in (0, 1):
            finish(routed, way, i)
        return carry

    lax.fori_loop(0, pieces, drain, 0)
    for way in (0, 1):
        finish(shared, way, 0)


def layer(x, w, gate, up, down, sgate, sup, sdown, n, g):
    rows, width = x.shape[2:]
    experts = w.shape[3]
    local, _, hidden = gate.shape
    thin = hidden // g
    wire = BF16 if n <= 4 else F32
    sliced = thin % 128 != 0
    if sliced:
        e = lax.axis_index("expert")
        sgate = lax.dynamic_slice_in_dim(sgate, e * thin, thin, 1)
        sup = lax.dynamic_slice_in_dim(sup, e * thin, thin, 1)
        sdown = lax.dynamic_slice_in_dim(sdown, e * thin, thin, 0)
    count = n * g * PITCH
    tiles = count // TILE
    slots = TILE // PITCH * CAP
    blocks = local * (hidden // COLS // 2)
    pieces = blocks * tiles * (slots // ROWS)
    half = n * g * rows // 2
    return pl.pallas_call(
        functools.partial(layer_kernel, n, g, sliced),
        out_shape=jax.ShapeDtypeStruct((n, g, rows, width), F32),
        in_specs=[VMEM] * 2 + [HBM] * 6,
        out_specs=VMEM,
        scratch_shapes=[
            pltpu.VMEM((count, width), BF16),
            pltpu.VMEM((count, experts), F32),
            pltpu.VMEM((local, width, hidden), BF16),
            pltpu.VMEM((local, width, hidden), BF16),
            pltpu.VMEM((local, hidden, width), BF16),
            pltpu.VMEM((width, thin), BF16),
            pltpu.VMEM((width, thin), BF16),
            pltpu.VMEM((thin, width), BF16),
            pltpu.VMEM((tiles, slots, width), BF16),
            pltpu.VMEM((TILE // PITCH * rows, width), BF16),
            pltpu.VMEM((count, hidden), BF16),
            pltpu.VMEM((count, thin), BF16),
            pltpu.VMEM((count, width), F32),
            pltpu.VMEM((local, count, 1), F32),
            pltpu.VMEM((2, pieces, 2, ROWS, COLS), F32),
            pltpu.VMEM((2, pieces, 2, ROWS, COLS), wire),
            pltpu.VMEM((2, pieces, 2, ROWS, COLS) if wire == BF16 else (8, 128), wire),
            pltpu.VMEM((2, pieces, ROWS, COLS), BF16),
            pltpu.VMEM((2, 1, 2, half, thin), F32),
            pltpu.VMEM((2, 1, 2, half, thin), wire),
            pltpu.VMEM((2, 1, 2, half, thin), wire),
            pltpu.VMEM((2, 1, half, thin), BF16),
            pltpu.VMEM((tiles, local, slots, TILE), BF16),
            pltpu.VMEM((tiles, local, TILE, slots), BF16),
            DMA((2, blocks)), DMA((local,)), DMA((3,)),
            DMA((2, pieces)), DMA((2, pieces)), DMA((2, pieces)), DMA((2, pieces)),
            DMA((2, 1)), DMA((2, 1)), DMA((2, 1)), DMA((2, 1)),
        ],
        compiler_params=params(1, 67043328),
    )(x, w, gate, up, down, sgate, sup, sdown)


def collect_kernel(n, g, y, o, peer_in, z, ship, plane, done, sa, ra, sb, rb, sc, rc, own):
    d, e, t = lax.axis_index("dp"), lax.axis_index("expert"), lax.axis_index("tensor")
    other = 1 - t
    half = n // 2
    width = y.shape[3]

    def goal(block):
        return o.at[:, pl.ds(pl.multiple_of(block * width, 128), width)]

    greet(
        [{"tensor": other}]
        + [{"expert": lax.rem(e + j, g)} for j in range(1, g)]
        + [{"dp": lax.rem(d + k, n), "tensor": c} for k in range(1, n) for c in (0, 1)]
    )
    order = list(range(1, g)) + [0]
    swap = {}
    for j in order:
        to = lax.rem(e + j, g)
        swap[j] = remote(
            y.at[pl.ds(other * half, half), to], peer_in.at[to], sa.at[j], ra.at[j], {"tensor": other}
        )
        swap[j].start()
    sends = []
    for j in order:
        to = lax.rem(e + j, g)
        swap[j].wait_recv()
        total = y[pl.ds(t * half, half), to] + peer_in[to]
        if j:
            ship[j] = packed(total, ship.dtype)
            copy = remote(ship.at[j], plane.at[j], sb.at[j], rb.at[j], {"expert": to})
            copy.start()
            sends.append(copy)
        else:
            z[...] = total
    total = z[...]
    for j in range(1, g):
        sends[j - 1].wait_recv()
        total = total + unpacked(plane[j])
    done[...] = total.astype(done.dtype)
    last = []
    for i in range(half):
        home = t * half + i
        for c in (0, 1):
            here = (home == d) & (t == c)
            away = remote(
                done.at[i], goal(d), sc.at[i, c], rc.at[d], {"dp": home, "tensor": c}
            )
            pl.when(jnp.logical_not(here))(away.start)
            local = pltpu.make_async_copy(done.at[i], goal(d), own)
            pl.when(here)(local.start)
            last.append((here, away, local))
    for k in range(n):
        local_arrives = (d // half == t) & (d == k)

        @pl.when(jnp.logical_not(local_arrives))
        def _():
            remote(done.at[0], goal(k), sc.at[0, 0], rc.at[k], {"dp": d}).wait_recv()

    for here, away, local in last:
        pl.when(jnp.logical_not(here))(away.wait_send)
        pl.when(here)(local.wait)
    for copy in list(swap.values()) + sends:
        copy.wait_send()


def collect(y, n, g):
    rows, width = y.shape[2:]
    half = n // 2
    wire = BF16 if n <= 4 else F32
    return pl.pallas_call(
        functools.partial(collect_kernel, n, g),
        out_shape=jax.ShapeDtypeStruct((rows, n * width), BF16),
        in_specs=[VMEM],
        out_specs=VMEM,
        scratch_shapes=[
            pltpu.VMEM((g, half, rows, width), F32),
            pltpu.VMEM((half, rows, width), F32),
            pltpu.VMEM((g, half, rows, width), wire),
            pltpu.VMEM((g, half, rows, width), wire),
            pltpu.VMEM((half, rows, width), BF16),
            DMA((g,)), DMA((g,)), DMA((g,)), DMA((g,)), DMA((half, 2)), DMA((n,)), DMA,
        ],
        compiler_params=params(2),
    )(y)


def per_device(
    tokens, expert_ids, route_weights, gate_weights, up_weights, down_weights,
    shared_gate, shared_up, shared_down,
):
    g, n = lax.axis_size("expert"), lax.axis_size("dp")
    experts = gate_weights.shape[0] * g
    x, w = dispatch(tokens, expert_ids, route_weights, experts, n, g)
    y = layer(
        x, w, gate_weights, up_weights, down_weights, shared_gate, shared_up, shared_down, n, g
    )
    return collect(y, n, g)


def solution(mesh):
    placed = (
        P(("dp", "expert"), None),
        P(("dp", "expert"), None),
        P(("dp", "expert"), None),
        P("expert", "dp", "tensor"),
        P("expert", "dp", "tensor"),
        P("expert", "tensor", "dp"),
        P("dp", "tensor"),
        P("dp", "tensor"),
        P("tensor", "dp"),
    )
    return jax.shard_map(
        per_device, mesh=mesh, in_specs=placed, out_specs=P(("dp", "expert"), None), check_vma=False
    )
```

time: 204 us -> 120 us (0.59)
  Pallas kernels: 161 us -> 114 us
  matrix products: 27.8 us -> 0 us
  local copies, waits for them, and re-layouts: 12.6 us -> 4.35 us
    pallas_call x1, Pallas kernels: 115 us -> 77.4 us  [layer(): pl.pallas_call(functools.partial(layer_kernel, n, g, sliced), out_shape=j...]
    dot_general x8 -> x0, matrix products: 27.8 us -> none  [the longest x1 9.08 us: per_device(): jnp.dot(spread.reshape(count, local * hidden), down_weights.reshape(local...]
    reshape x8 -> x0, local copies, waits for them, and re-layouts: 6.88 us -> none  [the longest x2 2.61 us: per_device(): x = x.reshape(count, width)]
    pallas_call x1, Pallas kernels: 24.6 us -> 19 us  [collect(): pl.pallas_call(functools.partial(collect_kernel, n, g), out_shape=jax.Sha...]
    pallas_call x1, Pallas kernels: 21.9 us -> 18 us  [dispatch(): pl.pallas_call(functools.partial(dispatch_kernel, n, g), out_shape=(jax.S...]
    unnamed x9 -> x3, local copies, waits for them, and re-layouts: 3.72 us -> 4.35 us
where the time goes in v1:
time: 120 us; the launch traced here: 119 us
  Pallas kernels  114 us (95%)
  local copies, waits for them, and re-layouts  4.35 us (4%)
    pallas_call x1, Pallas kernels, layer(): pl.pallas_call(functools.partial(layer_kernel, n, g, sliced), out_shape=j...  77.4 us
    pallas_call x1, Pallas kernels, collect(): pl.pallas_call(functools.partial(collect_kernel, n, g), out_shape=jax.Sha...  19 us
    pallas_call x1, Pallas kernels, dispatch(): pl.pallas_call(functools.partial(dispatch_kernel, n, g), out_shape=(jax.S...  18 us
    unnamed x3, local copies, waits for them, and re-layouts  4.35 us

profile of v1, /device:TPU:0, one launch (start us, length us, event | category | flops | bytes accessed | tf_op | source)
XLA Modules:
  0.0 118.9 jit_solution(9382356016233474666)
XLA Ops:
  0.0 1.4 %copy.10.ids = s32[12,8]{1,0:T(8,128)} copy(s32[12,8]{0,1:T(8,128)} %param.10) | data formatting | bytes 768 | tf_op args[1]
  1.4 1.3 %copy.11.weights = f32[12,8]{1,0:T(8,128)} copy(f32[12,8]{0,1:T(8,128)} %param.11) | data formatting | bytes 768 | tf_op args[2]
  2.7 18.0 %shard_map.91 = (bf16[4,4,12,1792]{3,2,1,0:T(8,128)(2,1)}, f32[4,4,12,16]{3,2,1,0:T(8,128)}) custom-call(bf16[12,7168]{1,0:T(8,128)(2,1)} %tok.1, s32[12,8]{1,0:T(8,128)} %copy.10.ids, f32[12,8]{1,0:T(8,128)} %copy.11.weights), custom_call_target="tpu_custom_call" | custom-call | tf_op jit(solution)/shard_map/pallas_call | solution.py:144
  20.8 77.4 %shard_map.92.y = f32[4,4,12,1792]{3,2,1,0:T(8,128)} custom-call(bf16[4,4,12,1792]{3,2,1,0:T(8,128)(2,1)} %get-tuple-element.7.x, f32[4,4,12,16]{3,2,1,0:T(8,128)} %get-tuple-element.8.w, bf16[4,1792,1024]{2,1,0:T(8,128)(2,1)} %gate.1, bf16[4,1792,1024]{2,1,0:T(8,128)(2,1)} %up.1, bf16[4,1024,1792]{2,1,0:T(8,128)(2,1)} %down.1, bf16[1792,1024]{1,0:T(8,128)(2,1)} %sgate.1, ...), custom_call_target="tpu_custom_call" | custom-call | tf_op jit(solution)/shard_map/pallas_call | solution.py:490
  98.2 19.0 %shard_map.93 = bf16[12,7168]{1,0:T(8,128)(2,1)} custom-call(f32[4,4,12,1792]{3,2,1,0:T(8,128)} %shard_map.92.y), custom_call_target="tpu_custom_call" | custom-call | tf_op jit(solution)/shard_map/pallas_call | solution.py:597
  117.2 1.6 %copy.13 = bf16[12,7168]{1,0:T(8,128)(2,1)} copy(bf16[12,7168]{1,0:T(8,128)(2,1)} %shard_map.93) | data formatting | bytes 344064

commit v2 on v1

--- a/solution.py
+++ b/solution.py
@@ -13,8 +13,8 @@
 COLS = 256
 ROWS = 64
 AHEAD = 3
-SKEW = 2
-SPREAD_SKEW = 2
+SKEW = 4
+SPREAD_SKEW = 5
 MESH = pl.DeviceIdType.MESH
 VMEM = pl.BlockSpec(memory_space=pltpu.VMEM)
 HBM = pl.BlockSpec(memory_space=pl.ANY)

time: 120 us -> 104 us (0.87)
  Pallas kernels: 114 us -> 99.4 us
    pallas_call x1, Pallas kernels: 77.4 us -> 64.3 us  [layer(): pl.pallas_call(functools.partial(layer_kernel, n, g, sliced), out_shape=j...]
    pallas_call x1, Pallas kernels: 19 us -> 17 us  [collect(): pl.pallas_call(functools.partial(collect_kernel, n, g), out_shape=jax.Sha...]
where the time goes in v2:
time: 104 us
  Pallas kernels  99.4 us (96%)
  local copies, waits for them, and re-layouts  4.35 us (4%)
    pallas_call x1, Pallas kernels, layer(): pl.pallas_call(functools.partial(layer_kernel, n, g, sliced), out_shape=j...  64.3 us
    pallas_call x1, Pallas kernels, dispatch(): pl.pallas_call(functools.partial(dispatch_kernel, n, g), out_shape=(jax.S...  18 us
    pallas_call x1, Pallas kernels, collect(): pl.pallas_call(functools.partial(collect_kernel, n, g), out_shape=jax.Sha...  17 us
    unnamed x3, local copies, waits for them, and re-layouts  4.35 us

profile of v2, /device:TPU:0, one launch (start us, length us, event | category | flops | bytes accessed | tf_op | source)
XLA Modules:
  0.0 103.8 jit_solution(11801370817287251247)
XLA Ops:
  0.0 1.4 %copy.10.ids = s32[12,8]{1,0:T(8,128)} copy(s32[12,8]{0,1:T(8,128)} %param.10) | data formatting | bytes 768 | tf_op args[1]
  1.4 1.3 %copy.11.weights = f32[12,8]{1,0:T(8,128)} copy(f32[12,8]{0,1:T(8,128)} %param.11) | data formatting | bytes 768 | tf_op args[2]
  2.7 18.0 %shard_map.91 = (bf16[4,4,12,1792]{3,2,1,0:T(8,128)(2,1)}, f32[4,4,12,16]{3,2,1,0:T(8,128)}) custom-call(bf16[12,7168]{1,0:T(8,128)(2,1)} %tok.1, s32[12,8]{1,0:T(8,128)} %copy.10.ids, f32[12,8]{1,0:T(8,128)} %copy.11.weights), custom_call_target="tpu_custom_call" | custom-call | tf_op jit(solution)/shard_map/pallas_call | solution.py:144
  20.8 64.3 %shard_map.92.y = f32[4,4,12,1792]{3,2,1,0:T(8,128)} custom-call(bf16[4,4,12,1792]{3,2,1,0:T(8,128)(2,1)} %get-tuple-element.7.x, f32[4,4,12,16]{3,2,1,0:T(8,128)} %get-tuple-element.8.w, bf16[4,1792,1024]{2,1,0:T(8,128)(2,1)} %gate.1, bf16[4,1792,1024]{2,1,0:T(8,128)(2,1)} %up.1, bf16[4,1024,1792]{2,1,0:T(8,128)(2,1)} %down.1, bf16[1792,1024]{1,0:T(8,128)(2,1)} %sgate.1, ...), custom_call_target="tpu_custom_call" | custom-call | tf_op jit(solution)/shard_map/pallas_call | solution.py:490
  85.1 17.0 %shard_map.93 = bf16[12,7168]{1,0:T(8,128)(2,1)} custom-call(f32[4,4,12,1792]{3,2,1,0:T(8,128)} %shard_map.92.y), custom_call_target="tpu_custom_call" | custom-call | tf_op jit(solution)/shard_map/pallas_call | solution.py:597
  102.1 1.6 %copy.13 = bf16[12,7168]{1,0:T(8,128)(2,1)} copy(bf16[12,7168]{1,0:T(8,128)(2,1)} %shard_map.93) | data formatting | bytes 344064

commit v3 on v2

v3 whole, which is shorter than its diff:
```python
import functools

import jax
import jax.numpy as jnp
from jax import lax
from jax.experimental import pallas as pl
from jax.experimental.pallas import tpu as pltpu
from jax.sharding import PartitionSpec as P

CAP = 8
PITCH = 16
TILE = 256
COLS = 256
ROWS = 64
AHEAD = 3
SKEW = 4
SPREAD_SKEW = 5
MESH = pl.DeviceIdType.MESH
VMEM = pl.BlockSpec(memory_space=pltpu.VMEM)
HBM = pl.BlockSpec(memory_space=pl.ANY)
DMA = pltpu.SemaphoreType.DMA
F32 = jnp.float32
BF16 = jnp.bfloat16


def greet(peers):
    barrier = pltpu.get_barrier_semaphore()
    for peer in peers:
        pl.semaphore_signal(barrier, inc=1, device_id=peer, device_id_type=MESH)
    pl.semaphore_wait(barrier, len(peers))


def remote(src, dst, send, recv, peer):
    return pltpu.make_async_remote_copy(
        src_ref=src, dst_ref=dst, send_sem=send, recv_sem=recv, device_id=peer, device_id_type=MESH
    )


def packed(v, wire):
    return v if wire == F32 else (v * jnp.abs(v)).astype(wire)


def unpacked(v):
    if v.dtype == F32:
        return v
    v = v.astype(F32)
    size = jnp.abs(v)
    root = size * lax.rsqrt(jnp.maximum(size, 1e-30))
    return jnp.where(v < 0.0, -root, root)


def dot(a, b):
    return jnp.dot(a, b, preferred_element_type=F32)


def layer_kernel(
    n, g, sliced, tok, ids, weights, gate, up, down, sgate, sup, sdown, o,
    x, w, coef, xs, ws, gbuf, ubuf, dbuf, sgbuf, subuf, sdbuf, picked, compact, spread, sspread, acc, factor,
    own, got, out, hid, sown, sgot, sout, shid, here, there, peer_in, kept, ship, plane, done,
    wsem, dsem, ssem, s1, r1, s2, r2, t1, q1, t2, q2,
    lsem, u1, v1, u2, v2, u3, v3, sa, ra, sb, rb, sc, rc, osem,
):
    d, e, t = lax.axis_index("dp"), lax.axis_index("expert"), lax.axis_index("tensor")
    other = 1 - t
    rows, width = x.shape[2:]
    experts = w.shape[3]
    local, hidden = gate.shape[0], gate.shape[2]
    thin = sgbuf.shape[1]
    wire = out.dtype
    tiles = xs.shape[0] // TILE
    slots = TILE // PITCH * CAP
    solid = TILE // PITCH * rows
    pairs = hidden // COLS // 2
    pieces = own.shape[1]
    blocks = local * pairs
    per = pieces // blocks
    place = (d, n - 1 - d)
    ahead = (jnp.minimum(d + 1, n - 1), jnp.maximum(d - 1, 0))
    behind = (jnp.maximum(d - 1, 0), jnp.minimum(d + 1, n - 1))

    def load(b):
        at, slot = b // pairs, lax.rem(b, gbuf.shape[0])
        wide = pl.ds(pl.multiple_of(lax.rem(b, pairs) * 2 * COLS, 2 * COLS), 2 * COLS)
        return [
            pltpu.make_async_copy(src.at[at, :, wide], dst.at[slot], wsem.at[h, b])
            for h, (src, dst) in enumerate(((gate, gbuf), (up, ubuf)))
        ]

    start = 0 if sliced else e * thin
    across = pl.ds(0, thin) if sliced else pl.ds(pl.multiple_of(start, thin), thin)
    extra = [
        pltpu.make_async_copy(sgate.at[:, across], sgbuf, ssem.at[0]),
        pltpu.make_async_copy(sup.at[:, across], subuf, ssem.at[1]),
        pltpu.make_async_copy(sdown.at[across, :], sdbuf, ssem.at[2]),
    ]
    lowers = [pltpu.make_async_copy(down.at[l], dbuf.at[l], dsem.at[l]) for l in range(local)]

    for copy in extra[:2]:
        copy.start()
    for b in range(min(AHEAD, blocks)):
        for copy in load(b):
            copy.start()

    split = (width // 2) % 128 == 0
    part_lanes = width // 2 if split else width
    lanes = pl.ds(pl.multiple_of(t * part_lanes, 128), part_lanes) if split else pl.ds(0, width)

    def columns(block, part):
        first = block * width + (t * part_lanes if part and split else 0)
        return tok.at[:, pl.ds(pl.multiple_of(first, 128), part_lanes if part else width)]

    mine = pltpu.make_async_copy(columns(d, False), x.at[d, e], lsem.at[0])
    mine.start()
    name = lax.broadcasted_iota(jnp.int32, coef.shape, 1)
    named, held = ids[...].T, weights[...].T
    total = jnp.zeros(coef.shape, F32)
    for k in range(ids.shape[0]):
        total = total + jnp.where(named[:, k:k + 1] == name, held[:, k:k + 1], 0.0)
    coef[...] = total
    greet(
        [{"tensor": other}]
        + [{"expert": lax.rem(e + j, g)} for j in range(1, g)]
        + [{"dp": lax.rem(d + k, n), "tensor": c} for k in range(1, n) for c in (0, 1)]
    )
    put = pltpu.make_async_copy(coef, w.at[d, e], lsem.at[1])
    put.start()
    sends = []
    for k in range(1, n):
        to = lax.rem(d + k, n)
        for src, dst, a in ((coef, w.at[d, e], 1), (columns(to, True), x.at[d, e, :, lanes], 0)):
            copy = remote(src, dst, u1.at[a, k], v1.at[a, k], {"dp": to})
            copy.start()
            sends.append(copy)

    def view(a, block, peer):
        return x.at[block, peer, :, lanes] if a == 0 else w.at[block, peer]

    def cross(k, j, block, peer):
        at = x.at[block, peer, :, lanes]
        return remote(at, at, u3.at[k, j], v3.at[k, j], {"tensor": other})

    xs[...] = jnp.zeros_like(xs)
    ws[...] = jnp.zeros_like(ws)
    for k in range(n):
        block = lax.rem(d - k + n, n)
        for a in (1, 0):
            if k == 0:
                (mine, put)[a].wait()
            else:
                at = view(a, block, e)
                remote(at, at, u1.at[a, k], v1.at[a, k], {"dp": d}).wait_recv()
            for j in range(1, g):
                at = view(a, block, e)
                copy = remote(at, at, u2.at[a, k, j], v2.at[a, k, j], {"expert": lax.rem(e + j, g)})
                copy.start()
                sends.append(copy)
        if split and k:
            copy = cross(k, 0, block, e)
            copy.start()
            sends.append(copy)

    def crossed(k, j, a):
        at = view(a, lax.rem(d - k + n, n), lax.rem(e - j + g, g))
        remote(at, at, u2.at[a, k, j], v2.at[a, k, j], {"expert": e}).wait_recv()

    for k in range(n):
        for j in range(1, g):
            crossed(k, j, 1)
    for i in range(n):
        for j in range(g):
            at = (i * g + j) * PITCH
            ws[at:at + rows, :] = w[i, j]

    def iota(shape, axis):
        return lax.broadcasted_iota(jnp.int32, shape, axis)

    token_row, token_col = iota((TILE, TILE), 0), iota((TILE, TILE), 1)
    same = token_row // PITCH == token_col // PITCH
    before = jnp.where(same & (token_row < token_col), 1.0, 0.0).astype(BF16)
    behind_in = jnp.where(same & (token_col < token_row), 1.0, 0.0).astype(BF16)
    spots = 16
    pick_rows = jnp.where(
        iota((spots, experts), 1) == e * local + iota((spots, experts), 0), 1.0, 0.0
    ).astype(BF16)
    base_row = iota((spots, TILE), 1) // PITCH * CAP
    base_col = iota((TILE, experts), 0) // PITCH * CAP
    for a in range(tiles):
        part = ws[a * TILE:(a + 1) * TILE, :]
        chosen = jnp.where(part > 0.0, 1.0, 0.0).astype(BF16)
        row = lax.dot_general(
            pick_rows, chosen, (((1,), (1,)), ((), ())), preferred_element_type=F32
        )
        rank_row = dot(row.astype(BF16), before).astype(jnp.int32)
        goal_row = jnp.where(row > 0.5, base_row + rank_row, -1)
        rank_col = dot(behind_in, chosen).astype(jnp.int32)
        goal_col = jnp.where(part > 0.0, base_col + rank_col, -1).astype(F32)
        for l in range(local):
            mark = iota((TILE, experts), 1) == e * local + l
            column = jnp.sum(jnp.where(mark, goal_col, 0.0), axis=1, keepdims=True)
            here[a, l] = jnp.where(
                goal_row[l:l + 1, :] == iota((slots, TILE), 0), 1.0, 0.0
            ).astype(BF16)
            there[a, l] = jnp.where(
                column.astype(jnp.int32) == iota((TILE, slots), 1), 1.0, 0.0
            ).astype(BF16)
            factor[l, a * TILE:(a + 1) * TILE, :] = jnp.sum(
                jnp.where(mark, part, 0.0), axis=1, keepdims=True
            )

    for k in range(n):
        for j in range(1, g):
            crossed(k, j, 0)
            if split:
                copy = cross(k, j, lax.rem(d - k + n, n), lax.rem(e - j + g, g))
                copy.start()
                sends.append(copy)
    if split:
        rest_lanes = pl.ds(pl.multiple_of(other * part_lanes, 128), part_lanes)
        for k in range(n):
            for j in range(g):
                if k or j:
                    at = x.at[lax.rem(d - k + n, n), lax.rem(e - j + g, g), :, rest_lanes]
                    remote(at, at, u3.at[k, j], v3.at[k, j], {"tensor": t}).wait_recv()
    for i in range(n):
        for j in range(g):
            at = (i * g + j) * PITCH
            xs[at:at + rows, :] = x[i, j]

    def solid_map(shape, slot_axis, token_axis):
        token, slot = iota(shape, token_axis), iota(shape, slot_axis)
        inside = token % PITCH
        return jnp.where(
            (inside < rows) & (token // PITCH * rows + inside == slot), 1.0, 0.0
        ).astype(BF16)

    rest = solid // 2
    pack_map = solid_map((solid, TILE), 0, 1)
    for a in range(tiles):
        compact[...] = dot(pack_map, xs[a * TILE:(a + 1) * TILE, :]).astype(BF16)
        if a == 0:
            for copy in extra[:2]:
                copy.wait()
        for h, buf in ((0, sgbuf), (1, subuf)):
            value = dot(compact[...], buf[...])
            for way in (0, 1):
                sown[way, 0, h, a * rest:(a + 1) * rest, :] = value[way * rest:(way + 1) * rest]

    routed = (own, got, out if wire == BF16 else own, hid, s1, r1, s2, r2)
    shared = (sown, sgot, sout if wire == BF16 else sown, shid, t1, q1, t2, q2)

    def partial_send(group, way, i):
        return remote(
            group[2].at[way, i], group[1].at[way, i], group[4].at[way, i], group[5].at[way, i],
            {"dp": ahead[way]},
        )

    def hidden_send(group, way, i):
        at = group[3].at[way, i]
        return remote(at, at, group[6].at[way, i], group[7].at[way, i], {"dp": behind[way]})

    def forward(group, way, i):
        mine, come, leave, final = group[:4]

        @pl.when(place[way] == 0)
        def _():
            if leave is not mine:
                for h in (0, 1):
                    leave[way, i, h] = packed(mine[way, i, h], wire)
            partial_send(group, way, i).start()

        @pl.when(place[way] > 0)
        def _():
            partial_send(group, way, i).wait_recv()

            @pl.when(place[way] < n - 1)
            def _():
                for h in (0, 1):
                    leave[way, i, h] = packed(mine[way, i, h] + unpacked(come[way, i, h]), wire)
                partial_send(group, way, i).start()

            @pl.when(place[way] == n - 1)
            def _():
                a, b = (mine[way, i, h] + unpacked(come[way, i, h]) for h in (0, 1))
                final[way, i] = (a / (1.0 + jnp.exp(-a)) * b).astype(final.dtype)
                hidden_send(group, way, i).start()

    def pass_on(group, way, i):
        hidden_send(group, way, i).wait_recv()

        @pl.when(place[way] > 0)
        def _():
            hidden_send(group, way, i).start()

    def project(b):
        at, slot = b // pairs, lax.rem(b, gbuf.shape[0])

        @pl.when(lax.rem(b, pairs) == 0)
        def _():
            for a in range(tiles):
                picked[a] = dot(here[a, at], xs[a * TILE:(a + 1) * TILE, :]).astype(BF16)

        for copy in load(b):
            copy.wait()

        @pl.when(b + AHEAD < blocks)
        def _():
            for copy in load(b + AHEAD):
                copy.start()

        @pl.when(b + AHEAD == blocks)
        def _():
            for copy in extra[2:] + lowers:
                copy.start()

        fine = slots // ROWS
        for way in (0, 1):
            for h, buf in ((0, gbuf), (1, ubuf)):
                for a in range(tiles):
                    value = dot(picked[a], buf[slot, :, way * COLS:(way + 1) * COLS])
                    for r in range(fine):
                        own[way, b * per + a * fine + r, h] = value[r * ROWS:(r + 1) * ROWS]

    def stage(b, carry):
        @pl.when(b < blocks)
        def _():
            project(b)

        for r in range(per):
            s = b * per + r
            for way in (0, 1):
                @pl.when(s == SKEW * place[way])
                def _():
                    forward(shared, way, 0)

                i = s - SKEW * place[way]

                @pl.when((i >= 0) & (i < pieces))
                def _():
                    forward(routed, way, i)
        return carry

    lax.fori_loop(0, blocks + -(-SKEW * (n - 1) // per), stage, 0)

    part_of = TILE if width % TILE == 0 else 128
    chunks = width // part_of
    ready = []

    def gather(l):
        for way in (0, 1):
            for c in range(pairs):
                b = l * pairs + c
                fine = slots // ROWS
                for a in range(tiles):
                    value = hid[way, b * per + a * fine:b * per + (a + 1) * fine]
                    spread[a * TILE:(a + 1) * TILE, (2 * c + way) * COLS:(2 * c + way + 1) * COLS] = dot(
                        there[a, l], value.reshape(slots, COLS)
                    ).astype(BF16)

    def shared_gather():
        unpack_map = solid_map((TILE, solid), 1, 0)
        for a in range(tiles):
            value = jnp.concatenate([shid[way, 0, a * rest:(a + 1) * rest] for way in (0, 1)], axis=0)
            sspread[a * TILE:(a + 1) * TILE, :] = dot(unpack_map, value).astype(BF16)

    deep = TILE // PITCH // g

    def shared_down(c):
        at = slice(c * part_of, (c + 1) * part_of)
        for a in range(tiles):
            span = slice(a * TILE, (a + 1) * TILE)
            value = dot(sspread[span, :], sdbuf[:, at])
            acc[a * deep:(a + 1) * deep, :, :, at] = value.reshape(deep, g, PITCH, part_of)

    def routed_down(l, c):
        at = slice(c * part_of, (c + 1) * part_of)
        for a in range(tiles):
            span = slice(a * TILE, (a + 1) * TILE)
            value = factor[l, span, :] * dot(spread[span, :], dbuf[l, :, at])
            acc[a * deep:(a + 1) * deep, :, :, at] += value.reshape(deep, g, PITCH, part_of)

    pool = n // 2
    cuts = [0, (chunks + 1) // 2, chunks]
    groups = [(cuts[q] * part_of, cuts[q + 1] * part_of) for q in (0, 1)]
    order = list(range(1, g)) + [0]

    def swap(q, j):
        lo, hi = groups[q]
        to = lax.rem(e + j, g)
        return remote(
            acc.at[pl.ds(other * pool, pool), to, :, pl.ds(lo, hi - lo)],
            peer_in.at[to, :, :, pl.ds(lo, hi - lo)], sa.at[q, j], ra.at[q, j], {"tensor": other},
        )

    def ship_to(q, j):
        lo, hi = groups[q]
        return remote(
            ship.at[j, :, :, pl.ds(lo, hi - lo)], plane.at[j, :, :, pl.ds(lo, hi - lo)],
            sb.at[q, j], rb.at[q, j], {"expert": lax.rem(e + j, g)},
        )

    def swap_out(q):
        for j in order:
            swap(q, j).start()

    def add_up(q):
        lo, hi = groups[q]
        for j in order:
            to = lax.rem(e + j, g)
            swap(q, j).wait_recv()
            value = acc[pl.ds(t * pool, pool), to, :, lo:hi] + peer_in[to, :, :, lo:hi]
            value = value[:, :rows]
            if j:
                ship[j, :, :, lo:hi] = packed(value, ship.dtype)
                ship_to(q, j).start()
            else:
                kept[:, :, lo:hi] = value

    def goal(q, block):
        lo, hi = groups[q]
        return o.at[:, pl.ds(pl.multiple_of(block * width + lo, 128), hi - lo)]

    def home_send(q, i):
        lo, hi = groups[q]
        home = t * pool + i
        src = done.at[i, :, pl.ds(lo, hi - lo)]
        copies = []
        for c in (0, 1):
            inside = (home == d) & (t == c)
            away = remote(src, goal(q, d), sc.at[q, i, c], rc.at[q, d], {"dp": home, "tensor": c})
            local_copy = pltpu.make_async_copy(src, goal(q, d), osem.at[q])
            copies.append((inside, away, local_copy))
        return copies

    def send_home(q):
        lo, hi = groups[q]
        value = kept[:, :, lo:hi]
        for j in range(1, g):
            ship_to(q, j).wait_recv()
            value = value + unpacked(plane[j, :, :, lo:hi])
        done[:, :, lo:hi] = value.astype(done.dtype)
        for i in range(pool):
            for inside, away, local_copy in home_send(q, i):
                pl.when(jnp.logical_not(inside))(away.start)
                pl.when(inside)(local_copy.start)

    def arrive(q):
        for k in range(n):
            stays = (d // pool == t) & (d == k)

            @pl.when(jnp.logical_not(stays))
            def _():
                lo, hi = groups[q]
                remote(
                    done.at[0, :, pl.ds(lo, hi - lo)], goal(q, k), sc.at[q, 0, 0], rc.at[q, k], {"dp": d}
                ).wait_recv()
        for i in range(pool):
            for inside, away, local_copy in home_send(q, i):
                pl.when(jnp.logical_not(inside))(away.wait_send)
                pl.when(inside)(local_copy.wait)
        for j in order:
            swap(q, j).wait_send()
            if j:
                ship_to(q, j).wait_send()

    lag = SPREAD_SKEW * (n - 2)
    each = pieces // local
    for s in range(pieces + lag):
        for way in (0, 1):
            late = n - 2 - place[way]

            @pl.when((late >= 0) & (s == SPREAD_SKEW * late))
            def _():
                pass_on(shared, way, 0)

            i = s - SPREAD_SKEW * late

            @pl.when((late >= 0) & (i >= 0) & (i < pieces))
            def _():
                pass_on(routed, way, i)
        if s == lag:
            def _start():
                extra[2].wait()
                shared_gather()
            ready.append(_start)
            ready += [functools.partial(shared_down, c) for c in range(chunks)]
        if s >= lag and (s - lag + 1) % each == 0:
            l = (s - lag + 1) // each - 1

            def _begin(l=l):
                lowers[l].wait()
                gather(l)
            ready.append(_begin)
            for c in range(chunks):
                ready.append(functools.partial(routed_down, l, c))
                if l == local - 1 and c + 1 in cuts:
                    ready.append(functools.partial(swap_out, cuts.index(c + 1) - 1))
        quota = 3 if s < pieces + lag - 1 else len(ready)
        for task in ready[:quota]:
            task()
        ready = ready[quota:]

    for stage_of in (add_up, send_home, arrive):
        for q in (0, 1):
            stage_of(q)

    def finish(group, way, i):
        @pl.when(place[way] < n - 1)
        def _():
            partial_send(group, way, i).wait_send()

        @pl.when(place[way] > 0)
        def _():
            hidden_send(group, way, i).wait_send()

    def drain(i, carry):
        for way in (0, 1):
            finish(routed, way, i)
        return carry

    lax.fori_loop(0, pieces, drain, 0)
    for way in (0, 1):
        finish(shared, way, 0)
    for copy in sends:
        copy.wait_send()


def layer(tokens, ids, weights, gate, up, down, sgate, sup, sdown, n, g):
    rows, model = tokens.shape
    width = model // n
    local, _, hidden = gate.shape
    experts = local * g
    thin = hidden // g
    wire = BF16 if n <= 4 else F32
    sliced = thin % 128 != 0
    if sliced:
        e = lax.axis_index("expert")
        sgate = lax.dynamic_slice_in_dim(sgate, e * thin, thin, 1)
        sup = lax.dynamic_slice_in_dim(sup, e * thin, thin, 1)
        sdown = lax.dynamic_slice_in_dim(sdown, e * thin, thin, 0)
    count = n * g * PITCH
    tiles = count // TILE
    slots = TILE // PITCH * CAP
    blocks = local * (hidden // COLS // 2)
    pieces = blocks * tiles * (slots // ROWS)
    half = n * g * rows // 2
    pool = n // 2
    ring = min(AHEAD + 1, blocks)
    return pl.pallas_call(
        functools.partial(layer_kernel, n, g, sliced),
        out_shape=jax.ShapeDtypeStruct((rows, model), BF16),
        in_specs=[VMEM] * 3 + [HBM] * 6,
        out_specs=VMEM,
        scratch_shapes=[
            pltpu.VMEM((n, g, rows, width), BF16),
            pltpu.VMEM((n, g, rows, experts), F32),
            pltpu.VMEM((rows, experts), F32),
            pltpu.VMEM((count, width), BF16),
            pltpu.VMEM((count, experts), F32),
            pltpu.VMEM((ring, width, 2 * COLS), BF16),
            pltpu.VMEM((ring, width, 2 * COLS), BF16),
            pltpu.VMEM((local, hidden, width), BF16),
            pltpu.VMEM((width, thin), BF16),
            pltpu.VMEM((width, thin), BF16),
            pltpu.VMEM((thin, width), BF16),
            pltpu.VMEM((tiles, slots, width), BF16),
            pltpu.VMEM((TILE // PITCH * rows, width), BF16),
            pltpu.VMEM((count, hidden), BF16),
            pltpu.VMEM((count, thin), BF16),
            pltpu.VMEM((n, g, PITCH, width), F32),
            pltpu.VMEM((local, count, 1), F32),
            pltpu.VMEM((2, pieces, 2, ROWS, COLS), F32),
            pltpu.VMEM((2, pieces, 2, ROWS, COLS), wire),
            pltpu.VMEM((2, pieces, 2, ROWS, COLS) if wire == BF16 else (8, 128), wire),
            pltpu.VMEM((2, pieces, ROWS, COLS), BF16),
            pltpu.VMEM((2, 1, 2, half, thin), F32),
            pltpu.VMEM((2, 1, 2, half, thin), wire),
            pltpu.VMEM((2, 1, 2, half, thin), wire),
            pltpu.VMEM((2, 1, half, thin), BF16),
            pltpu.VMEM((tiles, local, slots, TILE), BF16),
            pltpu.VMEM((tiles, local, TILE, slots), BF16),
            pltpu.VMEM((g, pool, PITCH, width), F32),
            pltpu.VMEM((pool, rows, width), F32),
            pltpu.VMEM((g, pool, rows, width), BF16),
            pltpu.VMEM((g, pool, rows, width), BF16),
            pltpu.VMEM((pool, rows, width), BF16),
            DMA((2, blocks)), DMA((local,)), DMA((3,)),
            DMA((2, pieces)), DMA((2, pieces)), DMA((2, pieces)), DMA((2, pieces)),
            DMA((2, 1)), DMA((2, 1)), DMA((2, 1)), DMA((2, 1)),
            DMA((2,)), DMA((2, n)), DMA((2, n)), DMA((2, n, g)), DMA((2, n, g)), DMA((n, g)), DMA((n, g)),
            DMA((2, g)), DMA((2, g)), DMA((2, g)), DMA((2, g)), DMA((2, pool, 2)), DMA((2, n)), DMA((2,)),
        ],
        compiler_params=pltpu.CompilerParams(
            collective_id=0, has_side_effects=True, vmem_limit_bytes=67043328
        ),
    )(tokens, ids, weights, gate, up, down, sgate, sup, sdown)


def per_device(
    tokens, expert_ids, route_weights, gate_weights, up_weights, down_weights,
    shared_gate, shared_up, shared_down,
):
    g, n = lax.axis_size("expert"), lax.axis_size("dp")
    return layer(
        tokens, expert_ids.T, route_weights.T, gate_weights, up_weights, down_weights,
        shared_gate, shared_up, shared_down, n, g,
    )


def solution(mesh):
    placed = (
        P(("dp", "expert"), None),
        P(("dp", "expert"), None),
        P(("dp", "expert"), None),
        P("expert", "dp", "tensor"),
        P("expert", "dp", "tensor"),
        P("expert", "tensor", "dp"),
        P("dp", "tensor"),
        P("dp", "tensor"),
        P("tensor", "dp"),
    )
    return jax.shard_map(
        per_device, mesh=mesh, in_specs=placed, out_specs=P(("dp", "expert"), None), check_vma=False
    )
```

time: 104 us -> 88.1 us (0.85)
  Pallas kernels: 99.4 us -> 86.3 us
  local copies, waits for them, and re-layouts: 4.35 us -> 1.64 us
    pallas_call x2 -> x0, Pallas kernels: 35.1 us -> none  [the longest x1 18 us: dispatch(): pl.pallas_call(functools.partial(dispatch_kernel, n, g), out_shape=(jax.S...]
    pallas_call x1, Pallas kernels: 64.3 us -> 86.3 us  [layer(): pl.pallas_call(functools.partial(layer_kernel, n, g, sliced), out_shape=j...]
    unnamed x3 -> x1, local copies, waits for them, and re-layouts: 4.35 us -> 1.64 us
where the time goes in v3:
time: 88.1 us; the launch traced here: 87.9 us
  Pallas kernels  86.3 us (98%)
  local copies, waits for them, and re-layouts  1.64 us (2%)
    pallas_call x1, Pallas kernels, layer(): pl.pallas_call(functools.partial(layer_kernel, n, g, sliced), out_shape=j...  86.3 us

profile of v3, /device:TPU:0, one launch (start us, length us, event | category | flops | bytes accessed | tf_op | source)
XLA Modules:
  0.0 87.9 jit_solution(13084951977834911103)
XLA Ops:
  0.0 86.3 %shard_map.91 = bf16[12,7168]{1,0:T(8,128)(2,1)} custom-call(bf16[12,7168]{1,0:T(8,128)(2,1)} %tok.1, s32[8,12]{1,0:T(8,128)} %bitcast.2, f32[8,12]{1,0:T(8,128)} %bitcast.3, bf16[4,1792,1024]{2,1,0:T(8,128)(2,1)} %gate.1, bf16[4,1792,1024]{2,1,0:T(8,128)(2,1)} %up.1, bf16[4,1024,1792]{2,1,0:T(8,128)(2,1)} %down.1, bf16[1792,1024]{1,0:T(8,128)(2,1)} %sgate.1, ...), custom_call_target="tpu_custom_call" | custom-call | tf_op jit(solution)/shard_map/pallas_call | solution.py:548
  86.3 1.6 %copy.11 = bf16[12,7168]{1,0:T(8,128)(2,1)} copy(bf16[12,7168]{1,0:T(8,128)(2,1)} %shard_map.91) | data formatting | bytes 344064

commit v4 on v3

--- a/solution.py
+++ b/solution.py
@@ -13,7 +13,7 @@
 COLS = 256
 ROWS = 64
 AHEAD = 3
-SKEW = 4
+SKEW = 5
 SPREAD_SKEW = 5
 MESH = pl.DeviceIdType.MESH
 VMEM = pl.BlockSpec(memory_space=pltpu.VMEM)
@@ -313,36 +313,36 @@
                 copy.start()
 
         fine = slots // ROWS
+        for h, buf in ((0, gbuf), (1, ubuf)):
+            for a in range(tiles):
+                value = dot(picked[a], buf[slot])
+                for way in (0, 1):
+                    for r in range(fine):
+                        own[way, b * per + a * fine + r, h] = value[
+                            r * ROWS:(r + 1) * ROWS, way * COLS:(way + 1) * COLS
+                        ]
+
+    def stage(s, carry):
+        @pl.when(s < blocks)
+        def _():
+            project(s)
+
         for way in (0, 1):
-            for h, buf in ((0, gbuf), (1, ubuf)):
-                for a in range(tiles):
-                    value = dot(picked[a], buf[slot, :, way * COLS:(way + 1) * COLS])
-                    for r in range(fine):
-                        own[way, b * per + a * fine + r, h] = value[r * ROWS:(r + 1) * ROWS]
-
-    def stage(b, carry):
-        @pl.when(b < blocks)
-        def _():
-            project(b)
-
-        for r in range(per):
-            s = b * per + r
-            for way in (0, 1):
-                @pl.when(s == SKEW * place[way])
-                def _():
-                    forward(shared, way, 0)
-
-                i = s - SKEW * place[way]
-
-                @pl.when((i >= 0) & (i < pieces))
-                def _():
-                    forward(routed, way, i)
+            @pl.when(s == SKEW * place[way])
+            def _():
+                forward(shared, way, 0)
+
+            i = s - SKEW * place[way]
+
+            @pl.when((i >= 0) & (i < pieces))
+            def _():
+                forward(routed, way, i)
         return carry
 
-    lax.fori_loop(0, blocks + -(-SKEW * (n - 1) // per), stage, 0)
-
-    part_of = TILE if width % TILE == 0 else 128
-    chunks = width // part_of
+    lax.fori_loop(0, pieces + SKEW * (n - 1), stage, 0)
+
+    spans = [(lo, min(lo + 2 * TILE, width)) for lo in range(0, width, 2 * TILE)]
+    chunks = len(spans)
     ready = []
 
     def gather(l):
@@ -365,22 +365,22 @@
     deep = TILE // PITCH // g
 
     def shared_down(c):
-        at = slice(c * part_of, (c + 1) * part_of)
+        at = slice(*spans[c])
         for a in range(tiles):
             span = slice(a * TILE, (a + 1) * TILE)
             value = dot(sspread[span, :], sdbuf[:, at])
-            acc[a * deep:(a + 1) * deep, :, :, at] = value.reshape(deep, g, PITCH, part_of)
+            acc[a * deep:(a + 1) * deep, :, :, at] = value.reshape(deep, g, PITCH, -1)
 
     def routed_down(l, c):
-        at = slice(c * part_of, (c + 1) * part_of)
+        at = slice(*spans[c])
         for a in range(tiles):
             span = slice(a * TILE, (a + 1) * TILE)
             value = factor[l, span, :] * dot(spread[span, :], dbuf[l, :, at])
-            acc[a * deep:(a + 1) * deep, :, :, at] += value.reshape(deep, g, PITCH, part_of)
+            acc[a * deep:(a + 1) * deep, :, :, at] += value.reshape(deep, g, PITCH, -1)
 
     pool = n // 2
-    cuts = [0, (chunks + 1) // 2, chunks]
-    groups = [(cuts[q] * part_of, cuts[q + 1] * part_of) for q in (0, 1)]
+    cuts = list(range(chunks + 1))
+    groups = spans
     order = list(range(1, g)) + [0]
 
     def swap(q, j):
@@ -500,7 +500,7 @@
         ready = ready[quota:]
 
     for stage_of in (add_up, send_home, arrive):
-        for q in (0, 1):
+        for q in range(chunks):
             stage_of(q)
 
     def finish(group, way, i):
@@ -545,6 +545,7 @@
     half = n * g * rows // 2
     pool = n // 2
     ring = min(AHEAD + 1, blocks)
+    parts = -(-width // (2 * TILE))
     return pl.pallas_call(
         functools.partial(layer_kernel, n, g, sliced),
         out_shape=jax.ShapeDtypeStruct((rows, model), BF16),
@@ -587,7 +588,8 @@
             DMA((2, pieces)), DMA((2, pieces)), DMA((2, pieces)), DMA((2, pieces)),
             DMA((2, 1)), DMA((2, 1)), DMA((2, 1)), DMA((2, 1)),
             DMA((2,)), DMA((2, n)), DMA((2, n)), DMA((2, n, g)), DMA((2, n, g)), DMA((n, g)), DMA((n, g)),
-            DMA((2, g)), DMA((2, g)), DMA((2, g)), DMA((2, g)), DMA((2, pool, 2)), DMA((2, n)), DMA((2,)),
+            DMA((parts, g)), DMA((parts, g)), DMA((parts, g)), DMA((parts, g)),
+            DMA((parts, pool, 2)), DMA((parts, n)), DMA((parts,)),
         ],
         compiler_params=pltpu.CompilerParams(
             collective_id=0, has_side_effects=True, vmem_limit_bytes=67043328

time: 88.1 us -> 86.8 us (0.985)
  Pallas kernels: 86.3 us -> 85 us
    pallas_call x1, Pallas kernels: 86.3 us -> 85 us  [layer(): pl.pallas_call(functools.partial(layer_kernel, n, g, sliced), out_shape=j...]
where the time goes in v4:
time: 86.8 us; the launch traced here: 86.7 us
  Pallas kernels  85 us (98%)
  local copies, waits for them, and re-layouts  1.64 us (2%)
    pallas_call x1, Pallas kernels, layer(): pl.pallas_call(functools.partial(layer_kernel, n, g, sliced), out_shape=j...  85 us

profile of v4, /device:TPU:0, one launch (start us, length us, event | category | flops | bytes accessed | tf_op | source)
XLA Modules:
  0.0 86.7 jit_solution(9315987833582614860)
XLA Ops:
  0.0 85.0 %shard_map.91 = bf16[12,7168]{1,0:T(8,128)(2,1)} custom-call(bf16[12,7168]{1,0:T(8,128)(2,1)} %tok.1, s32[8,12]{1,0:T(8,128)} %bitcast.2, f32[8,12]{1,0:T(8,128)} %bitcast.3, bf16[4,1792,1024]{2,1,0:T(8,128)(2,1)} %gate.1, bf16[4,1792,1024]{2,1,0:T(8,128)(2,1)} %up.1, bf16[4,1024,1792]{2,1,0:T(8,128)(2,1)} %down.1, bf16[1792,1024]{1,0:T(8,128)(2,1)} %sgate.1, ...), custom_call_target="tpu_custom_call" | custom-call | tf_op jit(solution)/shard_map/pallas_call | solution.py:549
  85.0 1.6 %copy.11 = bf16[12,7168]{1,0:T(8,128)(2,1)} copy(bf16[12,7168]{1,0:T(8,128)(2,1)} %shard_map.91) | data formatting | bytes 344064

commit v5 on v4

--- a/solution.py
+++ b/solution.py
@@ -13,7 +13,7 @@
 COLS = 256
 ROWS = 64
 AHEAD = 3
-SKEW = 5
+SKEW = 4
 SPREAD_SKEW = 5
 MESH = pl.DeviceIdType.MESH
 VMEM = pl.BlockSpec(memory_space=pltpu.VMEM)
@@ -68,6 +68,9 @@
     thin = sgbuf.shape[1]
     wire = out.dtype
     tiles = xs.shape[0] // TILE
+    pool, few = n // 2, n // 4
+    at_home = list(range(few)) + list(range(n - few, n)) + list(range(few, n - few))
+    position = [at_home.index(i) for i in range(n)]
     slots = TILE // PITCH * CAP
     solid = TILE // PITCH * rows
     pairs = hidden // COLS // 2
@@ -168,7 +171,7 @@
             crossed(k, j, 1)
     for i in range(n):
         for j in range(g):
-            at = (i * g + j) * PITCH
+            at = (position[i] * g + j) * PITCH
             ws[at:at + rows, :] = w[i, j]
 
     def iota(shape, axis):
@@ -200,9 +203,11 @@
             here[a, l] = jnp.where(
                 goal_row[l:l + 1, :] == iota((slots, TILE), 0), 1.0, 0.0
             ).astype(BF16)
-            there[a, l] = jnp.where(
-                column.astype(jnp.int32) == iota((TILE, slots), 1), 1.0, 0.0
-            ).astype(BF16)
+            for r in range(slots // ROWS):
+                piece = column[r * 2 * ROWS:(r + 1) * 2 * ROWS].astype(jnp.int32) - r * ROWS
+                there[a * (slots // ROWS) + r, l] = jnp.where(
+                    piece == iota((2 * ROWS, ROWS), 1), 1.0, 0.0
+                ).astype(BF16)
             factor[l, a * TILE:(a + 1) * TILE, :] = jnp.sum(
                 jnp.where(mark, part, 0.0), axis=1, keepdims=True
             )
@@ -223,7 +228,7 @@
                     remote(at, at, u3.at[k, j], v3.at[k, j], {"tensor": t}).wait_recv()
     for i in range(n):
         for j in range(g):
-            at = (i * g + j) * PITCH
+            at = (position[i] * g + j) * PITCH
             xs[at:at + rows, :] = x[i, j]
 
     def solid_map(shape, slot_axis, token_axis):
@@ -318,7 +323,7 @@
                 value = dot(picked[a], buf[slot])
                 for way in (0, 1):
                     for r in range(fine):
-                        own[way, b * per + a * fine + r, h] = value[
+                        own[way, (a * fine + r) * blocks + b, h] = value[
                             r * ROWS:(r + 1) * ROWS, way * COLS:(way + 1) * COLS
                         ]
 
@@ -345,15 +350,15 @@
     chunks = len(spans)
     ready = []
 
-    def gather(l):
-        for way in (0, 1):
-            for c in range(pairs):
-                b = l * pairs + c
-                fine = slots // ROWS
-                for a in range(tiles):
-                    value = hid[way, b * per + a * fine:b * per + (a + 1) * fine]
-                    spread[a * TILE:(a + 1) * TILE, (2 * c + way) * COLS:(2 * c + way + 1) * COLS] = dot(
-                        there[a, l], value.reshape(slots, COLS)
+    tall = 2 * ROWS
+    stack = tall // PITCH
+
+    def gather(r, l):
+        for u in range(r * per // 2, (r + 1) * per // 2):
+            for way in (0, 1):
+                for c in range(pairs):
+                    spread[u * tall:(u + 1) * tall, (2 * c + way) * COLS:(2 * c + way + 1) * COLS] = dot(
+                        there[u, l], hid[way, u * blocks + l * pairs + c]
                     ).astype(BF16)
 
     def shared_gather():
@@ -362,67 +367,73 @@
             value = jnp.concatenate([shid[way, 0, a * rest:(a + 1) * rest] for way in (0, 1)], axis=0)
             sspread[a * TILE:(a + 1) * TILE, :] = dot(unpack_map, value).astype(BF16)
 
-    deep = TILE // PITCH // g
-
     def shared_down(c):
         at = slice(*spans[c])
-        for a in range(tiles):
-            span = slice(a * TILE, (a + 1) * TILE)
-            value = dot(sspread[span, :], sdbuf[:, at])
-            acc[a * deep:(a + 1) * deep, :, :, at] = value.reshape(deep, g, PITCH, -1)
-
-    def routed_down(l, c):
+        for u in range(per):
+            value = dot(sspread[u * tall:(u + 1) * tall, :], sdbuf[:, at])
+            acc[u * stack:(u + 1) * stack, :, at] = value.reshape(stack, PITCH, -1)
+
+    def routed_down(r, l, c):
         at = slice(*spans[c])
-        for a in range(tiles):
-            span = slice(a * TILE, (a + 1) * TILE)
+        for u in range(r * per // 2, (r + 1) * per // 2):
+            span = slice(u * tall, (u + 1) * tall)
             value = factor[l, span, :] * dot(spread[span, :], dbuf[l, :, at])
-            acc[a * deep:(a + 1) * deep, :, :, at] += value.reshape(deep, g, PITCH, -1)
-
-    pool = n // 2
-    cuts = list(range(chunks + 1))
-    groups = spans
+            acc[u * stack:(u + 1) * stack, :, at] += value.reshape(stack, PITCH, -1)
+
+    middle = spans[(chunks - 1) // 2][1]
+    groups = [(0, 0, width), (1, 0, middle), (1, middle, width)]
     order = list(range(1, g)) + [0]
 
-    def swap(q, j):
-        lo, hi = groups[q]
+    def spot(r, core, i):
+        return r * pool + core * few + i
+
+    def home_of(r, core, i):
+        return few + core * few + i if r else core * (n - few) + i
+
+    def swap(q, j, i):
+        r, lo, hi = groups[q]
         to = lax.rem(e + j, g)
+        cols = pl.ds(lo, hi - lo)
         return remote(
-            acc.at[pl.ds(other * pool, pool), to, :, pl.ds(lo, hi - lo)],
-            peer_in.at[to, :, :, pl.ds(lo, hi - lo)], sa.at[q, j], ra.at[q, j], {"tensor": other},
+            acc.at[spot(r, other, i) * g + to, :, cols], peer_in.at[r, to, i, :, cols],
+            sa.at[q, j, i], ra.at[q, j, i], {"tensor": other},
         )
 
     def ship_to(q, j):
-        lo, hi = groups[q]
+        r, lo, hi = groups[q]
+        cols = pl.ds(lo, hi - lo)
         return remote(
-            ship.at[j, :, :, pl.ds(lo, hi - lo)], plane.at[j, :, :, pl.ds(lo, hi - lo)],
+            ship.at[r, j, :, :, cols], plane.at[r, j, :, :, cols],
             sb.at[q, j], rb.at[q, j], {"expert": lax.rem(e + j, g)},
         )
 
     def swap_out(q):
         for j in order:
-            swap(q, j).start()
+            for i in range(few):
+                swap(q, j, i).start()
 
     def add_up(q):
-        lo, hi = groups[q]
+        r, lo, hi = groups[q]
         for j in order:
             to = lax.rem(e + j, g)
-            swap(q, j).wait_recv()
-            value = acc[pl.ds(t * pool, pool), to, :, lo:hi] + peer_in[to, :, :, lo:hi]
-            value = value[:, :rows]
+            for i in range(few):
+                swap(q, j, i).wait_recv()
+                value = acc[spot(r, t, i) * g + to, :, lo:hi] + peer_in[r, to, i, :, lo:hi]
+                if j:
+                    ship[r, j, i, :, lo:hi] = packed(value[:rows], ship.dtype)
+                else:
+                    kept[r, i, :, lo:hi] = value[:rows]
             if j:
-                ship[j, :, :, lo:hi] = packed(value, ship.dtype)
                 ship_to(q, j).start()
-            else:
-                kept[:, :, lo:hi] = value
 
     def goal(q, block):
-        lo, hi = groups[q]
+        r, lo, hi = groups[q]
         return o.at[:, pl.ds(pl.multiple_of(block * width + lo, 128), hi - lo)]
 
     def home_send(q, i):
-        lo, hi = groups[q]
-        home = t * pool + i
-        src = done.at[i, :, pl.ds(lo, hi - lo)]
+        r, lo, hi = groups[q]
+        home = home_of(r, t, i)
+        src = done.at[r, i, :, pl.ds(lo, hi - lo)]
         copies = []
         for c in (0, 1):
             inside = (home == d) & (t == c)
@@ -432,38 +443,48 @@
         return copies
 
     def send_home(q):
-        lo, hi = groups[q]
-        value = kept[:, :, lo:hi]
+        r, lo, hi = groups[q]
         for j in range(1, g):
             ship_to(q, j).wait_recv()
-            value = value + unpacked(plane[j, :, :, lo:hi])
-        done[:, :, lo:hi] = value.astype(done.dtype)
-        for i in range(pool):
+        for i in range(few):
+            value = kept[r, i, :, lo:hi]
+            for j in range(1, g):
+                value = value + unpacked(plane[r, j, i, :, lo:hi])
+            done[r, i, :, lo:hi] = value.astype(done.dtype)
             for inside, away, local_copy in home_send(q, i):
                 pl.when(jnp.logical_not(inside))(away.start)
                 pl.when(inside)(local_copy.start)
 
+    inner = (d >= few) & (d < n - few)
+    upper = jnp.where(d >= pool, 1, 0)
+
     def arrive(q):
+        r, lo, hi = groups[q]
+        now = inner if r else jnp.logical_not(inner)
         for k in range(n):
-            stays = (d // pool == t) & (d == k)
-
-            @pl.when(jnp.logical_not(stays))
+            stays = (upper == t) & (d == k)
+
+            @pl.when(now & jnp.logical_not(stays))
             def _():
-                lo, hi = groups[q]
                 remote(
-                    done.at[0, :, pl.ds(lo, hi - lo)], goal(q, k), sc.at[q, 0, 0], rc.at[q, k], {"dp": d}
+                    done.at[r, 0, :, pl.ds(lo, hi - lo)], goal(q, k), sc.at[q, 0, 0], rc.at[q, k], {"dp": d}
                 ).wait_recv()
-        for i in range(pool):
+        for i in range(few):
             for inside, away, local_copy in home_send(q, i):
                 pl.when(jnp.logical_not(inside))(away.wait_send)
                 pl.when(inside)(local_copy.wait)
         for j in order:
-            swap(q, j).wait_send()
+            for i in range(few):
+                swap(q, j, i).wait_send()
             if j:
                 ship_to(q, j).wait_send()
 
     lag = SPREAD_SKEW * (n - 2)
-    each = pieces // local
+    later = [functools.partial(add_up, 0)]
+    due = {
+        ((r + 1) * per // 2 - 1) * blocks + (l + 1) * pairs - 1 + lag: (r, l)
+        for r in (0, 1) for l in range(local)
+    }
     for s in range(pieces + lag):
         for way in (0, 1):
             late = n - 2 - place[way]
@@ -483,25 +504,35 @@
                 shared_gather()
             ready.append(_start)
             ready += [functools.partial(shared_down, c) for c in range(chunks)]
-        if s >= lag and (s - lag + 1) % each == 0:
-            l = (s - lag + 1) // each - 1
-
-            def _begin(l=l):
-                lowers[l].wait()
-                gather(l)
+        if s in due:
+            r, l = due[s]
+
+            def _begin(r=r, l=l):
+                if r == 0:
+                    lowers[l].wait()
+                gather(r, l)
             ready.append(_begin)
             for c in range(chunks):
-                ready.append(functools.partial(routed_down, l, c))
-                if l == local - 1 and c + 1 in cuts:
-                    ready.append(functools.partial(swap_out, cuts.index(c + 1) - 1))
+                ready.append(functools.partial(routed_down, r, l, c))
+                if l == local - 1 and r == 1 and spans[c][1] in (middle, width):
+                    ready.append(functools.partial(swap_out, 1 if spans[c][1] == middle else 2))
+            if l == local - 1 and r == 0:
+                ready.append(functools.partial(swap_out, 0))
+            if r == 1 and l == 0 and local > 2:
+                ready.append(later.pop(0))
         quota = 3 if s < pieces + lag - 1 else len(ready)
         for task in ready[:quota]:
             task()
         ready = ready[quota:]
 
-    for stage_of in (add_up, send_home, arrive):
-        for q in range(chunks):
+    for task in later:
+        task()
+    send_home(0)
+    for stage_of in (add_up, send_home):
+        for q in (1, 2):
             stage_of(q)
+    for q in (0, 1, 2):
+        arrive(q)
 
     def finish(group, way, i):
         @pl.when(place[way] < n - 1)
@@ -543,9 +574,8 @@
     blocks = local * (hidden // COLS // 2)
     pieces = blocks * tiles * (slots // ROWS)
     half = n * g * rows // 2
-    pool = n // 2
+    few = n // 4
     ring = min(AHEAD + 1, blocks)
-    parts = -(-width // (2 * TILE))
     return pl.pallas_call(
         functools.partial(layer_kernel, n, g, sliced),
         out_shape=jax.ShapeDtypeStruct((rows, model), BF16),
@@ -567,7 +597,7 @@
             pltpu.VMEM((TILE // PITCH * rows, width), BF16),
             pltpu.VMEM((count, hidden), BF16),
             pltpu.VMEM((count, thin), BF16),
-            pltpu.VMEM((n, g, PITCH, width), F32),
+            pltpu.VMEM((n * g, PITCH, width), F32),
             pltpu.VMEM((local, count, 1), F32),
             pltpu.VMEM((2, pieces, 2, ROWS, COLS), F32),
             pltpu.VMEM((2, pieces, 2, ROWS, COLS), wire),
@@ -578,18 +608,18 @@
             pltpu.VMEM((2, 1, 2, half, thin), wire),
             pltpu.VMEM((2, 1, half, thin), BF16),
             pltpu.VMEM((tiles, local, slots, TILE), BF16),
-            pltpu.VMEM((tiles, local, TILE, slots), BF16),
-            pltpu.VMEM((g, pool, PITCH, width), F32),
-            pltpu.VMEM((pool, rows, width), F32),
-            pltpu.VMEM((g, pool, rows, width), BF16),
-            pltpu.VMEM((g, pool, rows, width), BF16),
-            pltpu.VMEM((pool, rows, width), BF16),
+            pltpu.VMEM((tiles * (slots // ROWS), local, 2 * ROWS, ROWS), BF16),
+            pltpu.VMEM((2, g, few, PITCH, width), F32),
+            pltpu.VMEM((2, few, rows, width), F32),
+            pltpu.VMEM((2, g, few, rows, width), BF16),
+            pltpu.VMEM((2, g, few, rows, width), BF16),
+            pltpu.VMEM((2, few, rows, width), BF16),
             DMA((2, blocks)), DMA((local,)), DMA((3,)),
             DMA((2, pieces)), DMA((2, pieces)), DMA((2, pieces)), DMA((2, pieces)),
             DMA((2, 1)), DMA((2, 1)), DMA((2, 1)), DMA((2, 1)),
             DMA((2,)), DMA((2, n)), DMA((2, n)), DMA((2, n, g)), DMA((2, n, g)), DMA((n, g)), DMA((n, g)),
-            DMA((parts, g)), DMA((parts, g)), DMA((parts, g)), DMA((parts, g)),
-            DMA((parts, pool, 2)), DMA((parts, n)), DMA((parts,)),
+            DMA((3, g, few)), DMA((3, g, few)), DMA((3, g)), DMA((3, g)),
+            DMA((3, few, 2)), DMA((3, n)), DMA((3,)),
         ],
         compiler_params=pltpu.CompilerParams(
             collective_id=0, has_side_effects=True, vmem_limit_bytes=67043328

time: 86.8 us -> 84.3 us (0.971)
  Pallas kernels: 85 us -> 82.5 us
    pallas_call x1, Pallas kernels: 85 us -> 82.5 us  [layer(): pl.pallas_call(functools.partial(layer_kernel, n, g, sliced), out_shape=j...]
where the time goes in v5:
time: 84.3 us; the launch traced here: 84.2 us
  Pallas kernels  82.5 us (98%)
  local copies, waits for them, and re-layouts  1.64 us (2%)
    pallas_call x1, Pallas kernels, layer(): pl.pallas_call(functools.partial(layer_kernel, n, g, sliced), out_shape=j...  82.5 us

profile of v5, /device:TPU:0, one launch (start us, length us, event | category | flops | bytes accessed | tf_op | source)
XLA Modules:
  0.0 84.2 jit_solution(12022649144361841115)
XLA Ops:
  0.0 82.5 %shard_map.91 = bf16[12,7168]{1,0:T(8,128)(2,1)} custom-call(bf16[12,7168]{1,0:T(8,128)(2,1)} %tok.1, s32[8,12]{1,0:T(8,128)} %bitcast.2, f32[8,12]{1,0:T(8,128)} %bitcast.3, bf16[4,1792,1024]{2,1,0:T(8,128)(2,1)} %gate.1, bf16[4,1792,1024]{2,1,0:T(8,128)(2,1)} %up.1, bf16[4,1024,1792]{2,1,0:T(8,128)(2,1)} %down.1, bf16[1792,1024]{1,0:T(8,128)(2,1)} %sgate.1, ...), custom_call_target="tpu_custom_call" | custom-call | tf_op jit(solution)/shard_map/pallas_call | solution.py:579
  82.5 1.6 %copy.11 = bf16[12,7168]{1,0:T(8,128)(2,1)} copy(bf16[12,7168]{1,0:T(8,128)(2,1)} %shard_map.91) | data formatting | bytes 344064
